TPU v7x, 32 devices: a whole 2x2x4 slice. The times are simulated.
32 devices in a mesh: dp: 16 (over z, y, x), mp: 2 (over core).
Axes of the slice: x: 2, y: 2, z: 4, core: 2. Of those that a mesh axis runs over, the one named last changes fastest.
Arguments:
- clean: float32 [64, 3, 4096], P(('dp', 'mp')), may hold values from -1 to 1
- noise: float32 [64, 3, 4096], P(('dp', 'mp')), may hold values from -12 to 12
- lowres: float32 [64, 3, 4096], P(('dp', 'mp')), may hold values from -1 to 1
- aug_noise: float32 [64, 3, 4096], P(('dp', 'mp')), may hold values from -5 to 5
- timesteps: int32 [64], P(('dp', 'mp')), may hold values from 0 to 999
- aug_levels: int32 [64], P(('dp', 'mp')), may hold values from 0 to 999
- lengths: int32 [64], P(('dp', 'mp')), may hold values from 1 to 128
- text: bfloat16 [64, 128, 4096], P(('dp', 'mp')), may hold values from -160 to 160
- w_stem: float32 [6, 128], replicated, may hold values from -2.5 to 2.5
- w_time: float32 [256, 256], replicated, may hold values from -0.375 to 0.375
- conv_one: bfloat16 [1152, 128], replicated, may hold values from -0.1875 to 0.1875
- conv_two: bfloat16 [1152, 128], replicated, may hold values from -0.1875 to 0.1875
- kv_weight: bfloat16 [4096, 256], P('mp'), may hold values from -0.09375 to 0.09375
- w_query: bfloat16 [128, 128], replicated, may hold values from -0.5 to 0.5
- w_output: bfloat16 [128, 128], replicated, may hold values from -0.5 to 0.5
- w_head: bfloat16 [3, 128], replicated, may hold values from -0.5 to 0.5
Outputs:
- conv_one_update: float32 [1152, 128], P(('dp', 'mp'))
- conv_two_update: float32 [1152, 128], P(('dp', 'mp'))
- kv_update: float32 [4096, 256], P('mp', 'dp')
- loss_mean: float32 [], replicated
All inputs are finite; a program needn't handle non-finite values.
Results may differ from a plain program's by a relative error of at most 0.03.
The roundings to bfloat16 on the way count: a program that leaves them out, or rounds other values in their place, can miss the bound.
Values may be sent and summed in bfloat16 or wider, within the bound.
A program may use at most 128 MiB of HBM per device.

v0:
```python
import functools
import math

import jax
import jax.numpy as jnp
from jax import lax
from jax.experimental import pallas as pl
from jax.experimental.pallas import tpu as pltpu
from jax.sharding import PartitionSpec as P

S = 64
GROUPS = 32
HEADS = 2
HEAD_DIM = 64
FREQS = 64
STEPS = 1000


def signal_level(index):
    ratio = (index.astype(jnp.float32) / STEPS + 0.008) / 1.008
    cosine = jnp.cos(ratio * (math.pi / 2.0))
    return cosine * cosine


def sinusoid(index):
    freqs = jnp.exp(-math.log(10000.0) * jnp.arange(FREQS, dtype=jnp.float32) / FREQS)
    angles = index.astype(jnp.float32) * freqs
    return jnp.concatenate([jnp.sin(angles), jnp.cos(angles)])


def prepare(clean, noise, lowres, aug_noise, tstep, level, w_stem, w_time):
    signal = signal_level(tstep)
    aug_signal = signal_level(level)
    noisy = jnp.sqrt(signal) * clean + jnp.sqrt(1.0 - signal) * noise
    low_noisy = jnp.sqrt(aug_signal) * lowres + jnp.sqrt(1.0 - aug_signal) * aug_noise
    stacked = jnp.concatenate([noisy, low_noisy], axis=0)
    h_start = jnp.einsum("kp,kc->pc", stacked, w_stem, precision=lax.Precision.HIGHEST)
    feature = jnp.concatenate([sinusoid(tstep), sinusoid(level)])[None, :]
    embed = jax.nn.silu(jnp.dot(feature, w_time, precision=lax.Precision.HIGHEST))[0]
    channels = w_stem.shape[1]
    return (h_start, embed[:channels], embed[channels:])


def group_matrix(channels):
    members = channels // GROUPS
    labels = jnp.arange(channels) // members
    return (labels[:, None] == labels[None, :]).astype(jnp.float32) / members


def group_norm(values, grouping):
    average = jnp.dot(
        jnp.mean(values, axis=0, keepdims=True), grouping, precision=lax.Precision.HIGHEST
    )
    centred = values - average
    spread = jnp.dot(
        jnp.mean(centred * centred, axis=0, keepdims=True),
        grouping,
        precision=lax.Precision.HIGHEST,
    )
    return centred * lax.rsqrt(spread + 1e-05)


def convolve(activation, weight):
    channels = weight.shape[1]
    kernel = weight.reshape(3, 3, channels, channels)
    picture = activation.reshape(1, S, S, channels)
    result = lax.conv_general_dilated(
        picture,
        kernel,
        (1, 1),
        "SAME",
        dimension_numbers=("NHWC", "HWIO", "NHWC"),
        preferred_element_type=jnp.float32,
    )
    return result.reshape(S * S, channels)


def image_loss(
    conv_one, conv_two, keys_values, h_start, scale, shift, keep, w_query, w_output, w_head, noise
):
    channels = conv_one.shape[1]
    grouping = group_matrix(channels)
    act_one = jax.nn.silu(group_norm(h_start, grouping)).astype(jnp.bfloat16)
    conv_out_one = convolve(act_one, conv_one)
    act_two = jax.nn.silu(group_norm(conv_out_one, grouping) * (1.0 + scale) + shift).astype(
        jnp.bfloat16
    )
    h_mid = h_start + convolve(act_two, conv_two)
    normed = group_norm(h_mid, grouping).astype(jnp.bfloat16)
    queries = (
        jnp.dot(normed, w_query, preferred_element_type=jnp.float32) * HEAD_DIM ** (-0.5)
    ).astype(jnp.bfloat16)
    width = w_query.shape[1]
    pieces = []
    for head_index in range(HEADS):
        lower = head_index * HEAD_DIM
        upper = lower + HEAD_DIM
        scores = jnp.dot(
            queries[:, lower:upper],
            keys_values[:, lower:upper].T,
            preferred_element_type=jnp.float32,
        )
        scores = jnp.where(keep[None, :], scores, -1e30)
        highest = jnp.max(scores, axis=1, keepdims=True)
        weights = jnp.exp(scores - highest)
        probs = (weights / jnp.sum(weights, axis=1, keepdims=True)).astype(jnp.bfloat16)
        pieces.append(
            jnp.dot(
                probs,
                keys_values[:, width + lower : width + upper],
                preferred_element_type=jnp.float32,
            )
        )
    attended = jnp.concatenate(pieces, axis=1).astype(jnp.bfloat16)
    h_out = h_mid + jnp.dot(attended, w_output, preferred_element_type=jnp.float32)
    pred = jnp.einsum(
        "kc,pc->kp", w_head, h_out.astype(jnp.bfloat16), preferred_element_type=jnp.float32
    )
    error = pred - noise
    return jnp.sum(error * error)


def exchange_kernel(
    n,
    mp_size,
    counts,
    conv_ref,
    kv_ref,
    loss_ref,
    conv_out,
    kv_out,
    stat_out,
    conv_in,
    kv_in,
    stat_in,
    stat_ref,
    conv_send,
    conv_recv,
    kv_send,
    kv_recv,
    stat_send,
    stat_recv,
):
    half = kv_out.shape[1]
    me = lax.axis_index("dp") * mp_size + lax.axis_index("mp")

    def target(k):
        return lax.rem(me + k + 1, n)

    def place(t):
        return (lax.div(t, mp_size), lax.rem(t, mp_size))

    def kv_block(t):
        column = pl.multiple_of(lax.rem(t, mp_size) * half, half)
        return kv_ref.at[lax.div(t, mp_size), :, pl.ds(column, half)]

    def remote(src, dst, send, recv, k, slot):
        return pltpu.make_async_remote_copy(
            src_ref=src,
            dst_ref=dst.at[slot],
            send_sem=send.at[k],
            recv_sem=recv.at[k],
            device_id=place(target(k)),
            device_id_type=pl.DeviceIdType.MESH,
        )

    def kv_copy(k):
        return remote(kv_block(target(k)), kv_in, kv_send, kv_recv, k, k)

    def conv_copy(k):
        return remote(conv_ref.at[target(k)], conv_in, conv_send, conv_recv, k, k)

    def stat_copy(k, slot):
        return remote(stat_ref, stat_in, stat_send, stat_recv, k, slot)

    def over_peers(step):
        def body(k, carry):
            step(k)
            return carry

        lax.fori_loop(0, n - 1, body, 0)

    barrier = pltpu.get_barrier_semaphore()
    over_peers(
        lambda k: pl.semaphore_signal(
            barrier,
            inc=1,
            device_id=place(target(k)),
            device_id_type=pl.DeviceIdType.MESH,
        )
    )
    pl.semaphore_wait(barrier, n - 1)

    def start(k):
        kv_copy(k).start()
        conv_copy(k).start()

    over_peers(start)
    own = pl.multiple_of(lax.rem(me, mp_size) * half, half)
    kv_out[...] = kv_ref[lax.div(me, mp_size), :, pl.ds(own, half)].astype(jnp.float32)
    conv_out[...] = conv_ref[me].astype(jnp.float32)

    def gather(k):
        kv_copy(k).wait_recv()
        kv_out[...] += kv_in[k].astype(jnp.float32)
        conv_copy(k).wait_recv()
        conv_out[...] += conv_in[k].astype(jnp.float32)

    over_peers(gather)

    def lanes(values):
        folded = jnp.sum(values * values, axis=0, keepdims=True)
        total = folded[:, :128]
        for piece in range(1, folded.shape[1] // 128):
            total = total + folded[:, piece * 128 : (piece + 1) * 128]
        return total

    stat_ref[...] = loss_ref[...]
    stat_ref[0:1, :] = lanes(conv_out[0])
    stat_ref[1:2, :] = lanes(conv_out[1])
    stat_ref[2:3, :] = lanes(kv_out[...])
    over_peers(lambda k: stat_copy(k, me).start())
    stat_in[me] = stat_ref[...]

    def add_stat(k):
        stat_copy(k, lax.rem(me + n - k - 1, n)).wait_recv()

    over_peers(add_stat)
    totals = jnp.sum(jnp.sum(stat_in[...], axis=0), axis=1, keepdims=True)
    stat_out[...] = jnp.broadcast_to(totals, stat_out.shape)
    conv_out[0] = conv_out[0] * lax.rsqrt(totals[0:1] / counts[0] + 1e-06)
    conv_out[1] = conv_out[1] * lax.rsqrt(totals[1:2] / counts[0] + 1e-06)
    kv_out[...] = kv_out[...] * lax.rsqrt(totals[2:3] / counts[1] + 1e-06)

    def finish(k):
        kv_copy(k).wait_send()
        conv_copy(k).wait_send()
        stat_copy(k, me).wait_send()

    over_peers(finish)


def exchange(conv_blocks, kv_blocks, loss, counts, mp_size):
    n = conv_blocks.shape[0]
    columns = kv_blocks.shape[1]
    half = kv_blocks.shape[2] // mp_size
    vmem = pl.BlockSpec(memory_space=pltpu.VMEM)
    return pl.pallas_call(
        functools.partial(exchange_kernel, n, mp_size, counts),
        out_shape=(
            jax.ShapeDtypeStruct(conv_blocks.shape[1:], jnp.float32),
            jax.ShapeDtypeStruct((columns, half), jnp.float32),
            jax.ShapeDtypeStruct(loss.shape, jnp.float32),
        ),
        in_specs=[vmem] * 3,
        out_specs=(vmem,) * 3,
        scratch_shapes=[
            pltpu.VMEM((n - 1,) + conv_blocks.shape[1:], conv_blocks.dtype),
            pltpu.VMEM((n - 1, columns, half), kv_blocks.dtype),
            pltpu.VMEM((n,) + loss.shape, jnp.float32),
            pltpu.VMEM(loss.shape, jnp.float32),
        ]
        + [pltpu.SemaphoreType.DMA((n - 1,))] * 6,
        compiler_params=pltpu.CompilerParams(collective_id=0, has_side_effects=True),
    )(conv_blocks, kv_blocks, loss)


def local(
    clean,
    noise,
    lowres,
    aug_noise,
    timesteps,
    aug_levels,
    lengths,
    text,
    w_stem,
    w_time,
    conv_one,
    conv_two,
    kv_weight,
    w_query,
    w_output,
    w_head,
):
    images = clean.shape[0]
    tokens = text.shape[1]
    features = text.shape[2]
    width = kv_weight.shape[1]
    half = kv_weight.shape[0]
    piece = lax.all_gather(kv_weight, "mp", axis=0, tiled=True)
    flat = jnp.dot(
        text.reshape(images * tokens, piece.shape[0]), piece, preferred_element_type=jnp.float32
    )
    summed = flat.reshape(images, tokens, width)
    keys_values = summed.astype(jnp.bfloat16)

    def one_image(items):
        clean_i, noise_i, low_i, aug_i, tstep, level, length, pairs = items
        h_start, scale, shift = prepare(
            clean_i, noise_i, low_i, aug_i, tstep, level, w_stem, w_time
        )
        keep = jnp.arange(tokens) < length
        value, pullback = jax.vjp(
            lambda first, second, third: image_loss(
                first,
                second,
                third,
                h_start,
                scale,
                shift,
                keep,
                w_query,
                w_output,
                w_head,
                noise_i,
            ),
            conv_one,
            conv_two,
            pairs,
        )
        part_one, part_two, part_kv = pullback(jnp.ones((), jnp.float32))
        return (part_one, part_two, part_kv, value)

    parts_one, parts_two, parts_kv, values = lax.map(
        one_image, (clean, noise, lowres, aug_noise, timesteps, aug_levels, lengths, keys_values)
    )
    local_one = jnp.sum(parts_one.astype(jnp.float32), axis=0)
    local_two = jnp.sum(parts_two.astype(jnp.float32), axis=0)
    dp_size = lax.axis_size("dp")
    mp_size = lax.axis_size("mp")
    devices = dp_size * mp_size
    turned = lax.dot_general(
        parts_kv.reshape(-1, width),
        text.reshape(-1, features),
        (((0,), (0,)), ((), ())),
        preferred_element_type=jnp.float32,
    ).astype(jnp.bfloat16)
    rows = conv_one.shape[0] // devices
    conv_blocks = jnp.stack(
        [
            local_one.reshape(devices, rows, conv_one.shape[1]),
            local_two.reshape(devices, rows, conv_one.shape[1]),
        ],
        axis=1,
    ).astype(jnp.bfloat16)
    loss = jnp.zeros((8, 128), jnp.float32).at[3, 0].set(jnp.sum(values))
    counts = (conv_one.shape[0] * conv_one.shape[1], half * mp_size * width)
    conv_updates, kv_turned, stats = exchange(
        conv_blocks,
        turned.reshape(dp_size, width // dp_size, features),
        loss,
        counts,
        mp_size,
    )
    loss_mean = stats[3, 0] / (images * devices * clean.shape[1] * clean.shape[2])
    return (conv_updates[0], conv_updates[1], kv_turned.T, loss_mean)


def solution(mesh):
    return jax.shard_map(
        local,
        mesh=mesh,
        in_specs=(
            P(("dp", "mp"), None, None),
            P(("dp", "mp"), None, None),
            P(("dp", "mp"), None, None),
            P(("dp", "mp"), None, None),
            P(("dp", "mp")),
            P(("dp", "mp")),
            P(("dp", "mp")),
            P(("dp", "mp"), None, None),
            P(),
            P(),
            P(),
            P(),
            P("mp", None),
            P(),
            P(),
            P(),
        ),
        out_specs=(P(("dp", "mp"), None), P(("dp", "mp"), None), P("mp", "dp"), P()),
        check_vma=False,
    )
```

profile of v0, /device:TPU:0, one launch (start us, length us, event | category | flops | bytes accessed | tf_op | source)
XLA Modules:
  0.0 313.5 jit_solution(10042923766533026229)
XLA Ops:
  8.0 14.8 %all-gather.2.cloned.1.call-done = bf16[4096,256]{1,0:T(8,128)(2,1)} async-done(((bf16[2048,256]{1,0:T(8,128)(2,1)}), bf16[4096,256]{1,0:T(8,128)(2,1)}) %all-gather.2.cloned.1.call-update) | async-done | bytes 2097168 | tf_op jit(solution)/shard_map/all_gather | solution.py:291
  22.9 3.0 fusion.284
  25.9 184.2 %while.20 = (s32[]{:T(128)}, bf16[2,1152,128]{2,1,0:T(8,128)(2,1)}, bf16[2,1152,128]{2,1,0:T(8,128)(2,1)}, bf16[2,128,256]{1,2,0:T(8,128)(2,1)}, f32[2]{0:T(128)...) while((s32[]{:T(128)}, bf16[2,1152,128]{2,1,0:T(8,128)(2,1)}, ...), condition=%wide.region_22.23_spmd, body=%wide.region_0.22_spmd.sunk | while | flops 8245876736 | bytes 325935616 | solution.py:325
  33.1 3.5 %fusion.462 = (f32[128]{0:T(128)S(1)}, f32[4096,128]{1,0:T(8,128)S(1)}) fusion(f32[6,128]{1,0:T(8,128)S(1)} %get-tuple-element.747, f32[3,4096]{1,0:T(4,128)S(1)} %fusion.460, f32[3,4096]{1,0:T(4,128)S(1)} %fusion.461), kind=kOutput, calls=%fused_computation.376.clone.1 | convolution fusion | flops 38297472 | bytes 2199040 | tf_op jit(solution)/shard_map/while/body/eval_jaxpr/kp,kc->pc/dot_general | solution.py:37
  40.1 3.0 select_reduce_fusion.8
  48.1 3.1 fusion.474
  58.0 2.1 convert_reduce_fusion.5
  62.4 2.1 convert_reduce_fusion.4
  65.6 1.5 convolution_convert_fusion.19
  67.1 4.3 %multiply_reduce_fusion.14 = (f32[]{:T(128)}, f32[3,4096]{1,0:T(4,128)}) fusion(f32[1,3,4096]{2,0,1:T(1,128)S(1)} %constant_dynamic-slice_fusion.8, bf16[3,128]{1,0:T(4,128)(2,1)} %get-tuple-element.755, f32[4096,128]{1,0:T(8,128)} %copy-done.1, bf16[128,128]{1,0:T(8,128)(2,1)} %get-tuple-element.754, ...), kind=kOutput, calls=%fused_computation.201.clone.1 | convolution fusion | flops 140546048 | bytes 3277572 | tf_op jit(solution)/shard_map/while/body/eval_jaxpr/jvp(kc,pc->kp)/dot_general | solution.py:116
  71.4 1.7 convolution_convert_fusion.21
  83.2 1.5 multiply_reduce_fusion.17
  89.2 5.1 %select_reduce_fusion.10 = (f32[128]{0:T(128)S(1)}, f32[64,8,9,128]{3,1,2,0:T(8,128)S(1)}) fusion(f32[64,8,9,128]{3,1,2,0:T(8,128)S(1)} %copy-done.8, f32[128]{0:T(128)S(1)} %copy-done.40, pred[8,9]{0,1:T(8,128)(4,1)} %get-tuple-element.830, f32[128]{0:T(128)S(1)} %copy-done.49, f32[128]{0:T(128)S(1)} %copy-done.47, f32[128]{0:T(128)S(1)} %copy-done.51, ...), kind=kOutput, calls=%fused_computation.51.clone.1 | convolution fusion | flops 1360920448 | bytes 6425160 | tf_op jit(solution)/shard_map/while/body/eval_jaxpr/transpose(jvp())/conv_general_dilated | solution.py:67
  99.3 5.0 %fusion.497 = bf16[3,3,128,128,1]{3,2,1,4,0:T(8,128)(2,1)S(1)} fusion(bf16[64,8,9,128,1]{3,1,4,2,0:T(8,128)(2,1)S(1)} %fusion.493, bf16[64,8,9,128,1]{3,1,4,2,0:T(8,128)(2,1)S(1)} %copy.117, bf16[64,8,9,128,1]{3,1,4,2,0:T(8,128)(2,1)S(1)} %fusion.494, f32[128]{0:T(128)S(1)} %fusion.496, pred[8,9]{0,1:T(8,128)(4,1)} %get-tuple-element.830, ...), kind=kOutput, calls=%fused_computation.101.clone.1 | convolution fusion | flops 1360281600 | bytes 8554568 | tf_op jit(solution)/shard_map/while/body/eval_jaxpr/transpose(jvp())/conv_general_dilated | solution.py:67
  104.4 1.8 fusion.489
  107.4 4.8 %fusion.490 = bf16[3,3,128,128,1]{3,2,1,4,0:T(8,128)(2,1)S(1)} fusion(bf16[64,8,9,128,1]{3,0,2,1,4:T(8,128)(2,1)S(1)} %bitcast.341, bf16[64,8,9,128,1]{3,1,2,0,4:T(8,128)(2,1)S(1)} %maximum_bitcast_fusion.8, bf16[64,8,9,128,1]{3,1,2,0,4:T(8,128)(2,1)S(1)} %fusion.489, bf16[64,8,9,128,1]{3,1,2,0,4:T(8,128)(2,1)S(1)} %maximum_bitcast_fusion.9), kind=kOutput, calls=%fused_computation.100.clone.1 | convolution fusion | flops 1348337664 | bytes 5013504 | tf_op jit(solution)/shard_map/while/body/eval_jaxpr/transpose(jvp())/conv_general_dilated | solution.py:67
  123.8 3.5 %fusion.462 = (f32[128]{0:T(128)S(1)}, f32[4096,128]{1,0:T(8,128)S(1)}) fusion(f32[6,128]{1,0:T(8,128)S(1)} %get-tuple-element.747, f32[3,4096]{1,0:T(4,128)S(1)} %fusion.460, f32[3,4096]{1,0:T(4,128)S(1)} %fusion.461), kind=kOutput, calls=%fused_computation.376.clone.1 | convolution fusion | flops 38297472 | bytes 2199040 | tf_op jit(solution)/shard_map/while/body/eval_jaxpr/kp,kc->pc/dot_general | solution.py:37
  130.9 3.0 select_reduce_fusion.8
  139.1 3.1 fusion.474
  149.0 2.1 convert_reduce_fusion.5
  153.4 2.1 convert_reduce_fusion.4
  156.6 1.5 convolution_convert_fusion.19
  158.0 4.3 %multiply_reduce_fusion.14 = (f32[]{:T(128)}, f32[3,4096]{1,0:T(4,128)}) fusion(f32[1,3,4096]{2,0,1:T(1,128)S(1)} %constant_dynamic-slice_fusion.8, bf16[3,128]{1,0:T(4,128)(2,1)} %get-tuple-element.755, f32[4096,128]{1,0:T(8,128)} %copy-done.1, bf16[128,128]{1,0:T(8,128)(2,1)} %get-tuple-element.754, ...), kind=kOutput, calls=%fused_computation.201.clone.1 | convolution fusion | flops 140546048 | bytes 3277572 | tf_op jit(solution)/shard_map/while/body/eval_jaxpr/jvp(kc,pc->kp)/dot_general | solution.py:116
  162.4 1.7 convolution_convert_fusion.21
  174.1 1.5 multiply_reduce_fusion.17
  180.1 4.9 %select_reduce_fusion.10 = (f32[128]{0:T(128)S(1)}, f32[64,8,9,128]{3,1,2,0:T(8,128)S(1)}) fusion(f32[64,8,9,128]{3,1,2,0:T(8,128)S(1)} %copy-done.8, f32[128]{0:T(128)S(1)} %copy-done.40, pred[8,9]{0,1:T(8,128)(4,1)} %get-tuple-element.830, f32[128]{0:T(128)S(1)} %copy-done.49, f32[128]{0:T(128)S(1)} %copy-done.47, f32[128]{0:T(128)S(1)} %copy-done.51, ...), kind=kOutput, calls=%fused_computation.51.clone.1 | convolution fusion | flops 1360920448 | bytes 6425160 | tf_op jit(solution)/shard_map/while/body/eval_jaxpr/transpose(jvp())/conv_general_dilated | solution.py:67
  190.0 5.0 %fusion.497 = bf16[3,3,128,128,1]{3,2,1,4,0:T(8,128)(2,1)S(1)} fusion(bf16[64,8,9,128,1]{3,1,4,2,0:T(8,128)(2,1)S(1)} %fusion.493, bf16[64,8,9,128,1]{3,1,4,2,0:T(8,128)(2,1)S(1)} %copy.117, bf16[64,8,9,128,1]{3,1,4,2,0:T(8,128)(2,1)S(1)} %fusion.494, f32[128]{0:T(128)S(1)} %fusion.496, pred[8,9]{0,1:T(8,128)(4,1)} %get-tuple-element.830, ...), kind=kOutput, calls=%fused_computation.101.clone.1 | convolution fusion | flops 1360281600 | bytes 8554568 | tf_op jit(solution)/shard_map/while/body/eval_jaxpr/transpose(jvp())/conv_general_dilated | solution.py:67
  195.1 1.8 fusion.489
  198.1 5.0 %fusion.490 = bf16[3,3,128,128,1]{3,2,1,4,0:T(8,128)(2,1)S(1)} fusion(bf16[64,8,9,128,1]{3,0,2,1,4:T(8,128)(2,1)S(1)} %bitcast.341, bf16[64,8,9,128,1]{3,1,2,0,4:T(8,128)(2,1)S(1)} %maximum_bitcast_fusion.8, bf16[64,8,9,128,1]{3,1,2,0,4:T(8,128)(2,1)S(1)} %fusion.489, bf16[64,8,9,128,1]{3,1,2,0,4:T(8,128)(2,1)S(1)} %maximum_bitcast_fusion.9), kind=kOutput, calls=%fused_computation.100.clone.1 | convolution fusion | flops 1348337664 | bytes 5013504 | tf_op jit(solution)/shard_map/while/body/eval_jaxpr/transpose(jvp())/conv_general_dilated | solution.py:67
  212.9 2.1 fusion.281
  217.7 82.8 %shard_map.183 = (f32[2,36,128]{2,1,0:T(8,128)}, f32[16,2048]{1,0:T(8,128)}, f32[8,128]{1,0:T(8,128)}) custom-call(bf16[32,2,36,128]{3,2,1,0:T(8,128)(2,1)} %pad_maximum_fusion.2.conv_ref, bf16[16,16,4096]{2,1,0:T(8,128)(2,1)} %bitcast.342, f32[8,128]{1,0:T(8,128)} %scatter.4.loss_ref), custom_call_target="tpu_custom_call" | custom-call | tf_op jit(solution)/shard_map/pallas_call | solution.py:248
  303.7 1.6 copy.149
  (467 shorter events, 101.0 us)
Async XLA Ops:
  7.2 15.7 %copy-start = (bf16[2,128,4096]{2,1,0:T(8,128)(2,1)S(1)}, bf16[2,128,4096]{2,1,0:T(8,128)(2,1)}, u32[]{:S(2)}) copy-start(bf16[2,128,4096]{2,1,0:T(8,128)(2,1)} %param.27) | copy-start | bytes 6291460
  7.2 15.7 %all-gather.2.cloned.1.call-start = ((), (), s32[]{:S(2)}) async-start(), calls=%async_computation | async-start | bytes 3145728 | tf_op jit(solution)/shard_map/all_gather | solution.py:291
  8.0 17.9 %copy-start.26 = (bf16[128,128]{1,0:T(8,128)(2,1)S(1)}, bf16[128,128]{1,0:T(8,128)(2,1)}, u32[]{:S(2)}) copy-start(bf16[128,128]{1,0:T(8,128)(2,1)} %param.33) | copy-start | bytes 98308
  8.0 17.9 %copy-start.30 = (pred[8,9]{0,1:T(8,128)(4,1)S(1)}, pred[8,9]{0,1:T(8,128)(4,1)}, u32[]{:S(2)}) copy-start(pred[8,9]{0,1:T(8,128)(4,1)} %constant.596) | copy-start | bytes 220
  8.0 17.8 %copy-start.54 = (f32[6,128]{1,0:T(8,128)S(1)}, f32[6,128]{1,0:T(8,128)}, u32[]{:S(2)}) copy-start(f32[6,128]{1,0:T(8,128)} %param.28) | copy-start | bytes 9220
  8.0 17.8 %copy-start.59 = (s32[2]{0:T(128)S(1)}, s32[2]{0:T(128)}, u32[]{:S(2)}) copy-start(s32[2]{0:T(128)} %param.24) | copy-start | bytes 28
  8.0 17.8 %copy-start.61 = (s32[2]{0:T(128)S(1)}, s32[2]{0:T(128)}, u32[]{:S(2)}) copy-start(s32[2]{0:T(128)} %param.25) | copy-start | bytes 28
  8.0 17.8 %copy-start.63 = (s32[2]{0:T(128)S(1)}, s32[2]{0:T(128)}, u32[]{:S(2)}) copy-start(s32[2]{0:T(128)} %param.26) | copy-start | bytes 28
  36.6 17.9 %copy-start.68 = (s32[128]{0:T(128)}, s32[128]{0:T(128)S(1)}, u32[]{:S(2)}) copy-start(s32[128]{0:T(128)S(1)} %and_select_fusion.2) | copy-start | bytes 1540 | tf_op jit(solution)/shard_map/while
  55.8 5.7 %copy-start.15 = (bf16[4096,128]{0,1:T(8,128)(2,1)}, bf16[4096,128]{0,1:T(8,128)(2,1)S(1)}, u32[]{:S(2)}) copy-start(bf16[4096,128]{0,1:T(8,128)(2,1)S(1)} %fusion.477) | copy-start | bytes 3145732 | tf_op jit(solution)/shard_map/while
  89.2 5.1 %copy-start.70 = (f32[128]{0:T(128)S(1)}, f32[128]{0:T(128)}, u32[]{:S(2)}) copy-start(f32[128]{0:T(128)} %get-tuple-element.677) | copy-start | bytes 1540 | tf_op jit(solution)/shard_map/while
  107.3 4.9 %copy-start.33 = (bf16[2,1152,128]{2,1,0:T(8,128)(2,1)S(1)}, bf16[2,1152,128]{2,1,0:T(8,128)(2,1)}, u32[]{:S(2)}) copy-start(bf16[2,1152,128]{2,1,0:T(8,128)(2,1)} %get-tuple-element.710) | copy-start | bytes 1769476 | tf_op jit(solution)/shard_map/while
  107.3 4.9 %copy-start.35 = (bf16[2,1152,128]{2,1,0:T(8,128)(2,1)S(1)}, bf16[2,1152,128]{2,1,0:T(8,128)(2,1)}, u32[]{:S(2)}) copy-start(bf16[2,1152,128]{2,1,0:T(8,128)(2,1)} %get-tuple-element.711) | copy-start | bytes 1769476 | tf_op jit(solution)/shard_map/while
  107.3 5.8 %copy-start.65 = (f32[2]{0:T(128)S(1)}, f32[2]{0:T(128)}, u32[]{:S(2)}) copy-start(f32[2]{0:T(128)} %get-tuple-element.713) | copy-start | bytes 28 | tf_op jit(solution)/shard_map/while
  107.3 7.1 %copy-start.27 = (bf16[128,128]{1,0:T(8,128)(2,1)S(1)}, bf16[128,128]{1,0:T(8,128)(2,1)}, u32[]{:S(2)}) copy-start(bf16[128,128]{1,0:T(8,128)(2,1)} %get-tuple-element.799) | copy-start | bytes 98308 | tf_op jit(solution)/shard_map/while
  107.3 7.1 %copy-start.31 = (pred[8,9]{0,1:T(8,128)(4,1)S(1)}, pred[8,9]{0,1:T(8,128)(4,1)}, u32[]{:S(2)}) copy-start(pred[8,9]{0,1:T(8,128)(4,1)} %get-tuple-element.830) | copy-start | bytes 220 | tf_op jit(solution)/shard_map/while
  107.3 7.1 %copy-start.55 = (f32[6,128]{1,0:T(8,128)S(1)}, f32[6,128]{1,0:T(8,128)}, u32[]{:S(2)}) copy-start(f32[6,128]{1,0:T(8,128)} %get-tuple-element.860) | copy-start | bytes 9220 | tf_op jit(solution)/shard_map/while
  107.3 7.1 %copy-start.60 = (s32[2]{0:T(128)S(1)}, s32[2]{0:T(128)}, u32[]{:S(2)}) copy-start(s32[2]{0:T(128)} %get-tuple-element.892) | copy-start | bytes 28 | tf_op jit(solution)/shard_map/while
  107.4 7.1 %copy-start.62 = (s32[2]{0:T(128)S(1)}, s32[2]{0:T(128)}, u32[]{:S(2)}) copy-start(s32[2]{0:T(128)} %get-tuple-element.924) | copy-start | bytes 28 | tf_op jit(solution)/shard_map/while
  107.4 7.1 %copy-start.64 = (s32[2]{0:T(128)S(1)}, s32[2]{0:T(128)}, u32[]{:S(2)}) copy-start(s32[2]{0:T(128)} %get-tuple-element.957) | copy-start | bytes 28 | tf_op jit(solution)/shard_map/while
  127.3 18.2 %copy-start.68 = (s32[128]{0:T(128)}, s32[128]{0:T(128)S(1)}, u32[]{:S(2)}) copy-start(s32[128]{0:T(128)S(1)} %and_select_fusion.2) | copy-start | bytes 1540 | tf_op jit(solution)/shard_map/while
  146.8 5.7 %copy-start.15 = (bf16[4096,128]{0,1:T(8,128)(2,1)}, bf16[4096,128]{0,1:T(8,128)(2,1)S(1)}, u32[]{:S(2)}) copy-start(bf16[4096,128]{0,1:T(8,128)(2,1)S(1)} %fusion.477) | copy-start | bytes 3145732 | tf_op jit(solution)/shard_map/while
  180.1 4.9 %copy-start.70 = (f32[128]{0:T(128)S(1)}, f32[128]{0:T(128)}, u32[]{:S(2)}) copy-start(f32[128]{0:T(128)} %get-tuple-element.677) | copy-start | bytes 1540 | tf_op jit(solution)/shard_map/while
  198.0 5.1 %copy-start.33 = (bf16[2,1152,128]{2,1,0:T(8,128)(2,1)S(1)}, bf16[2,1152,128]{2,1,0:T(8,128)(2,1)}, u32[]{:S(2)}) copy-start(bf16[2,1152,128]{2,1,0:T(8,128)(2,1)} %get-tuple-element.710) | copy-start | bytes 1769476 | tf_op jit(solution)/shard_map/while
  198.0 5.1 %copy-start.35 = (bf16[2,1152,128]{2,1,0:T(8,128)(2,1)S(1)}, bf16[2,1152,128]{2,1,0:T(8,128)(2,1)}, u32[]{:S(2)}) copy-start(bf16[2,1152,128]{2,1,0:T(8,128)(2,1)} %get-tuple-element.711) | copy-start | bytes 1769476 | tf_op jit(solution)/shard_map/while
  198.0 6.1 %copy-start.65 = (f32[2]{0:T(128)S(1)}, f32[2]{0:T(128)}, u32[]{:S(2)}) copy-start(f32[2]{0:T(128)} %get-tuple-element.713) | copy-start | bytes 28 | tf_op jit(solution)/shard_map/while
  198.0 7.4 %copy-start.27 = (bf16[128,128]{1,0:T(8,128)(2,1)S(1)}, bf16[128,128]{1,0:T(8,128)(2,1)}, u32[]{:S(2)}) copy-start(bf16[128,128]{1,0:T(8,128)(2,1)} %get-tuple-element.799) | copy-start | bytes 98308 | tf_op jit(solution)/shard_map/while
  198.0 7.4 %copy-start.31 = (pred[8,9]{0,1:T(8,128)(4,1)S(1)}, pred[8,9]{0,1:T(8,128)(4,1)}, u32[]{:S(2)}) copy-start(pred[8,9]{0,1:T(8,128)(4,1)} %get-tuple-element.830) | copy-start | bytes 220 | tf_op jit(solution)/shard_map/while
  198.0 7.4 %copy-start.55 = (f32[6,128]{1,0:T(8,128)S(1)}, f32[6,128]{1,0:T(8,128)}, u32[]{:S(2)}) copy-start(f32[6,128]{1,0:T(8,128)} %get-tuple-element.860) | copy-start | bytes 9220 | tf_op jit(solution)/shard_map/while
  198.1 7.3 %copy-start.60 = (s32[2]{0:T(128)S(1)}, s32[2]{0:T(128)}, u32[]{:S(2)}) copy-start(s32[2]{0:T(128)} %get-tuple-element.892) | copy-start | bytes 28 | tf_op jit(solution)/shard_map/while
  198.1 7.3 %copy-start.62 = (s32[2]{0:T(128)S(1)}, s32[2]{0:T(128)}, u32[]{:S(2)}) copy-start(s32[2]{0:T(128)} %get-tuple-element.924) | copy-start | bytes 28 | tf_op jit(solution)/shard_map/while
  198.1 7.3 %copy-start.64 = (s32[2]{0:T(128)S(1)}, s32[2]{0:T(128)}, u32[]{:S(2)}) copy-start(s32[2]{0:T(128)} %get-tuple-element.957) | copy-start | bytes 28 | tf_op jit(solution)/shard_map/while
  (104 other events, 180.0 us)
Sparse Core Ops, SparseCore 0:
  9.5 13.2 all-gather.1
where the time goes:
time: 316 us; the launch traced here: 313 us
  matrix products  96.3 us (30%)
  Pallas kernels  82.8 us (26%)
  local copies, waits for them, and re-layouts  52.8 us (17%)
  other arithmetic  36.8 us (12%)
  between operations  16.2 us (5%)
  waiting for transfers between devices  15.5 us (5%)
  loops' own time  13.1 us (4%)
    pallas_call x1, Pallas kernels, exchange(): pl.pallas_call(functools.partial(exchange_kernel, n, mp_size, counts), ou...  82.8 us
    conv_general_dilated x10, matrix products, convolve(): lax.conv_general_dilated(picture, kernel, (1, 1), 'SAME', dimension_numbe...  42 us
    while x260, local copies, waits for them, and re-layouts  19.4 us
    all_gather x1, waiting for transfers between devices, local(): piece = lax.all_gather(kv_weight, 'mp', axis=0, tiled=True)  14.8 us
    another operation x1, loops' own time, local(): lax.map(one_image, (clean, noise, lowres, aug_noise, timesteps, aug_level...  13.1 us
    dot_general x4, matrix products, image_loss(): jnp.einsum('kc,pc->kp', w_head, h_out.astype(jnp.bfloat16), preferred_ele...  12.1 us
    dynamic_slice x14, local copies, waits for them, and re-layouts, local(): lax.map(one_image, (clean, noise, lowres, aug_noise, timesteps, aug_level...  11.3 us
    dot_general x12, matrix products, image_loss(): jnp.dot(probs, keys_values[:, width + lower:width + upper], preferred_ele...  10.3 us
  transfers between devices with their start and end apart: 1, of which 1 were waited for; matrix products, arithmetic and copies ran while one was open for 0% of the time, Pallas kernels for 0%

commit v1 on v0

v1 whole, which is shorter than its diff:
```python
import functools
import math

import jax
import jax.numpy as jnp
from jax import lax
from jax.experimental import pallas as pl
from jax.experimental.pallas import tpu as pltpu
from jax.sharding import PartitionSpec as P

S = 64
GROUPS = 32
HEADS = 2
HEAD_DIM = 64
FREQS = 64
STEPS = 1000
F32 = jnp.float32
BF16 = jnp.bfloat16
EPS = 1e-05
TAPS = 3


def level_of(index):
    ratio = (index / STEPS + 0.008) / 1.008
    cosine = jnp.cos(ratio * (math.pi / 2.0))
    return cosine * cosine


def dot(a, b):
    return jnp.dot(a, b, preferred_element_type=F32)


def dot_lhs_t(a, b):
    return lax.dot_general(a, b, (((0,), (0,)), ((), ())), preferred_element_type=F32)


def dot_rhs_t(a, b):
    return lax.dot_general(a, b, (((1,), (1,)), ((), ())), preferred_element_type=F32)


def fold(values):
    rows, lanes = values.shape
    return jnp.sum(values.reshape(rows // 8, 8, lanes), axis=0)


def group_mean(acc, count):
    total = jnp.sum(acc, axis=0, keepdims=True)
    channels = acc.shape[1]
    total = jnp.broadcast_to(total, acc.shape)
    lane = lax.broadcasted_iota(jnp.int32, acc.shape, 1)
    members = channels // GROUPS
    step = 1
    while step < members:
        up = pltpu.roll(total, channels - step, 1)
        down = pltpu.roll(total, step, 1)
        total = total + jnp.where((lane // step) % 2 == 0, up, down)
        step *= 2
    return total[0:1] / (count * members)


def sigmoid(x):
    return 1.0 / (1.0 + jnp.exp(-x))


def split3(x):
    one = x.astype(BF16).astype(F32)
    two = (x - one).astype(BF16).astype(F32)
    three = (x - one - two).astype(BF16).astype(F32)
    return one, two, three


def radices_of(size):
    parts = []
    for step in (2, 2):
        if size % step == 0 and size > 1:
            parts.append(step)
            size //= step
    while size > 1:
        step = next((s for s in (4, 2, 3, 5, 7) if size % s == 0), size)
        parts.append(step)
        size //= step
    return tuple(parts)


def blocks_of(shape, radices):
    return [tuple(reversed(radices[j:])) + tuple(shape) for j in range(len(radices))]


def lands_of(shape, radices, dp_size, mp_size):
    lands = [(mp_size - 1, dp_size) + tuple(shape)]
    for j, radix in enumerate(radices):
        lands.append((radix - 1,) + tuple(reversed(radices[j + 1 :])) + tuple(shape))
    return lands


def scratch_of(shape, radices, dp_size, mp_size):
    copies = mp_size - 1 + sum(r - 1 for r in radices)
    return (
        [pltpu.VMEM(s, BF16) for s in blocks_of(shape, radices)]
        + [pltpu.VMEM(s, BF16) for s in lands_of(shape, radices, dp_size, mp_size)]
        + [pltpu.SemaphoreType.DMA((copies,)), pltpu.SemaphoreType.DMA((copies,))]
    )


class Scatter:
    def __init__(self, pick, read, final, radices, refs, dp_size, mp_size):
        k = len(radices)
        self.pick, self.read, self.final, self.radices = pick, read, final, radices
        self.sums, self.lands = refs[:k], refs[k : 2 * k + 1]
        self.send, self.recv = refs[2 * k + 1 :]
        self.dp_size, self.mp_size = dp_size, mp_size
        self.dp, self.mp = lax.axis_index("dp"), lax.axis_index("mp")
        self.place = []
        stride = 1
        for radix in radices:
            self.place.append((lax.rem(lax.div(self.dp, stride), radix), stride))
            stride *= radix

    def copies(self, j):
        out = []
        if j == 0:
            for k in range(self.mp_size - 1):
                peer = lax.rem(self.mp + k + 1, self.mp_size)
                out.append((self.pick(peer), self.lands[0].at[k], k, (self.dp, peer)))
        else:
            radix = self.radices[j - 1]
            digit, stride = self.place[j - 1]
            first = self.mp_size - 1 + sum(r - 1 for r in self.radices[: j - 1])
            rest = len(self.radices) - j
            for k in range(radix - 1):
                there = lax.rem(digit + k + 1, radix)
                src = self.sums[j - 1].at[(slice(None),) * rest + (there,)]
                peer = self.dp + (there - digit) * stride
                out.append((src, self.lands[j].at[k], first + k, (peer, self.mp)))
        return [
            pltpu.make_async_remote_copy(
                src_ref=src,
                dst_ref=dst,
                send_sem=self.send.at[sem],
                recv_sem=self.recv.at[sem],
                device_id=peer,
                device_id_type=pl.DeviceIdType.MESH,
            )
            for src, dst, sem, peer in out
        ]

    def start(self, j):
        for copy in self.copies(j):
            copy.start()

    def finish(self, j):
        for copy in self.copies(j):
            copy.wait_recv()
        count = len(self.lands[j].shape)
        total = 1
        shape = tuple(reversed(self.radices[j:]))
        for s in shape:
            total *= s
        for flat in range(total):
            at, left = [], flat
            for s in reversed(shape):
                at.insert(0, left % s)
                left //= s
            at = tuple(at)
            if j == 0:
                value = self.read(flat, self.mp)
                lands = [self.lands[0][k, flat] for k in range(self.mp_size - 1)]
            else:
                digit = self.place[j - 1][0]
                value = self.sums[j - 1][at + (digit,)].astype(F32)
                lands = [self.lands[j][(k,) + at] for k in range(self.radices[j - 1] - 1)]
            for land in lands:
                value = value + land.astype(F32)
            if j < len(self.radices):
                self.sums[j][at] = value.astype(BF16)
            else:
                self.final[...] = value

    def drain(self):
        for j in range(len(self.radices) + 1):
            for copy in self.copies(j):
                copy.wait_send()


def block_kernel(n, mp_size, kv_radices, conv_radices, last_radices, *refs):
    (
        tsteps,
        levels,
        lengths,
        clean,
        noise,
        lowres,
        aug_noise,
        text,
        kv_weight,
        w_stem,
        w_time,
        conv_one,
        conv_two,
        w_query,
        w_output,
        w_head,
        one_out,
        two_out,
        kv_out,
        stat_out,
        emb_ref,
        kv_ref,
        cot_ref,
        kt_ref,
        kd_ref,
        vd_ref,
        vt_ref,
        wq_t,
        wo_t,
        wt_two,
        wh_ref,
        stem_lhs,
        noise_ref,
        norms,
        h_ref,
        xs_ref,
        a_one,
        a_two,
        gx_ref,
        c_ref,
        hm_ref,
        go_ref,
        dn_ref,
        g_one,
        acc_w,
        acc_k,
        acc_v,
        grad_one,
        grad_two,
        kv_land,
        kv_send,
        kv_recv,
        stat_ref,
        stat_land,
        stat_send,
        stat_recv,
        kv_blocks,
        one_blocks,
        two_blocks,
    ) = refs[:59]
    rest = refs[59:]
    sizes = [2 * len(r) + 3 for r in (kv_radices, last_radices, conv_radices)]
    kv_refs = rest[: sizes[0]]
    one_refs = rest[sizes[0] : sizes[0] + sizes[1]]
    two_refs = rest[sizes[0] + sizes[1] :]

    images, tokens, features = text.shape
    pixels = clean.shape[2]
    channels, width = w_query.shape
    span = TAPS * channels
    heads = w_head.shape[0]
    half = kv_weight.shape[0]
    dp_size = n // mp_size
    big = 1024
    mid = 1024
    count = float(pixels)
    my_dp, my_mp = lax.axis_index("dp"), lax.axis_index("mp")
    me = my_dp * mp_size + my_mp

    def place(t):
        return (lax.div(t, mp_size), lax.rem(t, mp_size))

    def over_peers(step):
        lax.fori_loop(0, n - 1, lambda k, c: (step(k), c)[1], 0)

    def target(k):
        return lax.rem(me + k + 1, n)

    barrier = pltpu.get_barrier_semaphore()
    over_peers(
        lambda k: pl.semaphore_signal(
            barrier, inc=1, device_id=place(target(k)), device_id_type=pl.DeviceIdType.MESH
        )
    )

    def chunks(size, body, init=0):
        return lax.fori_loop(0, pixels // size, lambda i, c: body(pl.multiple_of(i * size, size), c), init)

    zero8 = jnp.zeros((8, channels), F32)

    wq_t[...] = w_query[...].astype(F32).T.astype(BF16)
    wo_t[...] = w_output[...].astype(F32).T.astype(BF16)
    for dy in range(TAPS):
        for dx in range(TAPS):
            src = (TAPS * (TAPS - 1 - dy) + (TAPS - 1 - dx)) * channels
            dst = (TAPS * dy + dx) * channels
            wt_two[dst : dst + channels, :] = conv_two[src : src + channels, :].astype(F32).T.astype(BF16)
    wh_ref[...] = jnp.zeros_like(wh_ref)
    wh_ref[0:heads, :] = w_head[...].astype(F32)
    wh_ref[8 : 8 + heads, :] = w_head[...].astype(F32)
    wh = wh_ref[...].astype(BF16)
    stem_lhs[...] = jnp.zeros_like(stem_lhs)
    noise_ref[...] = jnp.zeros_like(noise_ref)
    stem_lhs[0, 0 : w_stem.shape[0], 0:channels] = w_stem[...]
    s1, s2, s3 = split3(stem_lhs[0, :, 0:channels])
    stem_w = jnp.concatenate([s1, s2, s1, s2, s3, s1], axis=0).astype(BF16)
    edge = jnp.zeros((S, span), BF16)
    for i in range(images):
        for ref in (a_one, a_two, gx_ref):
            ref[i, 0:S, :] = edge
            ref[i, S + pixels :, :] = edge
        t = jnp.full((8, 128), tsteps[i].astype(F32), F32)
        a = jnp.full((8, 128), levels[i].astype(F32), F32)
        signal, aug_signal = level_of(t), level_of(a)
        k1, k2 = jnp.sqrt(signal)[0:1, 0:1], jnp.sqrt(1.0 - signal)[0:1, 0:1]
        k3, k4 = jnp.sqrt(aug_signal)[0:1, 0:1], jnp.sqrt(1.0 - aug_signal)[0:1, 0:1]
        for k in range(heads):
            row = noise[k, i : i + 1, :]
            noise_ref[i, k : k + 1, :] = row
            stem_lhs[i, k : k + 1, :] = k1 * clean[k, i : i + 1, :] + k2 * row
            stem_lhs[i, heads + k : heads + k + 1, :] = k3 * lowres[k, i : i + 1, :] + k4 * aug_noise[k, i : i + 1, :]
    g_one[0:S, :] = edge[:, :channels]
    g_one[S + pixels :, :] = edge[:, :channels]
    grad_one[...] = jnp.zeros_like(grad_one)
    grad_two[...] = jnp.zeros_like(grad_two)

    lane = lax.broadcasted_iota(jnp.int32, (8, 4 * FREQS), 1)
    row = lax.broadcasted_iota(jnp.int32, (8, 4 * FREQS), 0)
    base = jnp.zeros((8, 4 * FREQS), F32)
    for i in range(images):
        both = jnp.where(lane < 2 * FREQS, tsteps[i].astype(F32), levels[i].astype(F32))
        base = jnp.where(row == i, both, base)
    freqs = jnp.exp(-math.log(10000.0) * (lane % FREQS).astype(F32) / FREQS)
    angles = base * freqs
    feature = jnp.where((lane // FREQS) % 2 == 0, jnp.sin(angles), jnp.cos(angles))
    emb = jnp.dot(feature, w_time[...], precision=lax.Precision.HIGHEST, preferred_element_type=F32)
    emb = emb * sigmoid(emb)
    for i in range(images):
        emb_ref[i] = jnp.broadcast_to(emb[i : i + 1], emb.shape)

    pl.semaphore_wait(barrier, n - 1)

    def kv_copy(k):
        return pltpu.make_async_remote_copy(
            src_ref=kv_weight,
            dst_ref=kv_land.at[k],
            send_sem=kv_send.at[k],
            recv_sem=kv_recv.at[k],
            device_id=(my_dp, lax.rem(my_mp + k + 1, mp_size)),
            device_id_type=pl.DeviceIdType.MESH,
        )

    for k in range(mp_size - 1):
        kv_copy(k).start()

    def shifted(dst, r0, size):
        x = lax.broadcasted_iota(jnp.int32, (size, channels), 0) % S
        window = xs_ref.at[pl.ds(r0, size + 16), :]
        left = window[7 : 7 + size, :]
        here = window[8 : 8 + size, :]
        right = window[9 : 9 + size, :]
        rows = pl.ds(r0 + S, size)
        dst[rows, 0:channels] = jnp.where(x == 0, 0.0, left).astype(BF16)
        dst[rows, channels : 2 * channels] = here.astype(BF16)
        dst[rows, 2 * channels : span] = jnp.where(x == S - 1, 0.0, right).astype(BF16)

    def convolve(src, weight, r0, size):
        total = None
        for dy in range(TAPS):
            part = dot(src[pl.ds(r0 + dy * S, size), :], weight[dy * span : (dy + 1) * span, :])
            total = part if total is None else total + part
        return total

    def weight_grad(src, g_src, lane0, grad):
        acc_w[...] = jnp.zeros_like(acc_w)

        def body(r0, carry):
            g = jnp.concatenate(
                [g_src[pl.ds(r0 + (2 - dy) * S, big), lane0 : lane0 + channels] for dy in range(TAPS)], axis=1
            )
            acc_w[...] += dot_lhs_t(src[pl.ds(r0 + S, big), :], g)
            return carry

        chunks(big, body)
        for dy in range(TAPS):
            part = acc_w[:, dy * channels : (dy + 1) * channels]
            grad[dy * span : (dy + 1) * span, :] += part.astype(BF16).astype(F32)

    def variance(ref, mean):
        def body(r0, acc):
            d = ref[pl.ds(r0, big), :] - mean
            return acc + fold(d * d)

        return lax.rsqrt(group_mean(chunks(big, body, zero8), count) + EPS)

    def keep_row(i, k, value):
        norms[i, k] = jnp.broadcast_to(value, (8, channels))

    def row_of(i, k):
        return norms[i, k, 0:1, :]

    def gain_bias(i):
        return 1.0 + emb_ref[i, 0:1, 0:channels], emb_ref[i, 0:1, channels : 2 * channels]

    def forward(i, carry):
        def stem(r0, acc):
            x1, x2, x3 = split3(stem_lhs[i, :, pl.ds(r0, big)])
            x = jnp.concatenate([x1, x1, x2, x2, x1, x3], axis=0).astype(BF16)
            h = dot_lhs_t(x, stem_w)
            h_ref[pl.ds(r0, big), :] = h
            return acc + fold(h)

        m1 = group_mean(chunks(big, stem, zero8), count)
        r1 = variance(h_ref, m1)

        def act_one(r0, c):
            x = (h_ref[pl.ds(r0, big), :] - m1) * r1
            xs_ref[pl.ds(r0 + 8, big), :] = x * sigmoid(x)
            return c

        one, two, conv, mid_map = a_one.at[i], a_two.at[i], c_ref.at[i], hm_ref.at[i]
        chunks(big, act_one)
        chunks(big, lambda r0, c: (shifted(one, r0, big), c)[1])

        def conv1(r0, acc):
            c = convolve(one, conv_one, r0, big)
            conv[pl.ds(r0, big), :] = c
            return acc + fold(c)

        m2 = group_mean(chunks(big, conv1, zero8), count)
        r2 = variance(conv, m2)
        gain, bias = gain_bias(i)

        def act_two(r0, c):
            z = (conv[pl.ds(r0, big), :] - m2) * r2 * gain + bias
            xs_ref[pl.ds(r0 + 8, big), :] = z * sigmoid(z)
            return c

        chunks(big, act_two)
        chunks(big, lambda r0, c: (shifted(two, r0, big), c)[1])

        def conv2(r0, acc):
            h = h_ref[pl.ds(r0, big), :] + convolve(two, conv_two, r0, big)
            mid_map[pl.ds(r0, big), :] = h
            return acc + fold(h)

        m3 = group_mean(chunks(big, conv2, zero8), count)
        r3 = variance(mid_map, m3)
        for k, value in enumerate((m2, r2, m3, r3)):
            keep_row(i, k, value)
        return carry

    lax.fori_loop(0, images, forward, 0)

    def features_of(m):
        cols = pl.ds(pl.multiple_of(m * half, half), half)
        return text[:, :, cols].reshape(images * tokens, half)

    kv = dot(features_of(my_mp), kv_weight[...])
    for k in range(mp_size - 1):
        kv_copy(k).wait_recv()
        kv += dot(features_of(lax.rem(my_mp + mp_size - k - 1, mp_size)), kv_land[k])
    kv_ref[...] = kv.astype(BF16).reshape(images, tokens, 2 * width)

    lane_w = lax.broadcasted_iota(jnp.int32, (tokens, width), 1)

    def attend(i, square):
        m3, r3 = row_of(i, 2), row_of(i, 3)
        keys = kv_ref[i, :, 0:width].astype(F32)
        values = kv_ref[i, :, width : 2 * width].astype(F32)
        for h in range(HEADS):
            mine = (lane_w // HEAD_DIM) == h
            k_h = jnp.where(mine, keys, 0.0)
            v_h = jnp.where(mine, values, 0.0)
            rows = slice(h * tokens, (h + 1) * tokens)
            kt_ref[:, rows] = k_h.T.astype(BF16)
            kd_ref[rows, :] = k_h.astype(BF16)
            vd_ref[rows, :] = v_h.astype(BF16)
            vt_ref[:, rows] = v_h.T.astype(BF16)
        acc_k[...] = jnp.zeros_like(acc_k)
        acc_v[...] = jnp.zeros_like(acc_v)
        length = lengths[i]
        scale = HEAD_DIM**-0.5
        mid_map = hm_ref.at[i]

        def attention(r0, carry):
            s1, s2, sq = carry
            rows = pl.ds(r0, mid)
            hm = mid_map[rows, :]
            xh = (hm - m3) * r3
            q = (dot(xh.astype(BF16), w_query[...]) * scale).astype(BF16)
            scores = dot(q, kt_ref[...])
            keep = lax.broadcasted_iota(jnp.int32, (mid, tokens), 1) < length
            probs = []
            for h in range(HEADS):
                s = jnp.where(keep, scores[:, h * tokens : (h + 1) * tokens], -1e30)
                w = jnp.exp(s - jnp.max(s, axis=1, keepdims=True))
                probs.append(w * (1.0 / jnp.sum(w, axis=1, keepdims=True)))
            pb = jnp.concatenate([p.astype(BF16) for p in probs], axis=1)
            attended = dot(pb, vd_ref[...]).astype(BF16)
            hob = (hm + dot(attended, w_output[...])).astype(BF16)
            error = dot_rhs_t(wh[0:8], hob) - noise_ref[i, :, rows]
            sq = sq + error * error
            e2 = error * 2.0
            high = e2.astype(BF16).astype(F32)
            e2 = jnp.concatenate([high, e2 - high], axis=0).astype(BF16)
            g = dot_lhs_t(e2, wh).astype(BF16)
            go_ref[rows, :] = g
            d_att = dot(g, wo_t[...]).astype(BF16)
            d_probs = dot(d_att, vt_ref[...]).astype(BF16).astype(F32)
            acc_v[...] += dot_lhs_t(pb, d_att)
            d_scores = []
            for h in range(HEADS):
                t = d_probs[:, h * tokens : (h + 1) * tokens] * probs[h]
                d_scores.append((t - probs[h] * jnp.sum(t, axis=1, keepdims=True)).astype(BF16))
            ds = jnp.concatenate(d_scores, axis=1)
            acc_k[...] += dot_lhs_t(ds, q)
            d_q = dot(ds, kd_ref[...]).astype(BF16)
            dn = (dot(d_q, wq_t[...]) * scale).astype(BF16)
            dn_ref[rows, :] = dn
            dx = dn.astype(F32)
            return s1 + fold(dx), s2 + fold(dx * xh), sq

        s1, s2, square = chunks(mid, attention, (zero8, zero8, square))
        n1, n2 = group_mean(s1, count), group_mean(s2, count)
        first = lane_w < HEAD_DIM
        cot_ref[i, :, 0:width] = jnp.where(first, acc_k[0:tokens, :], acc_k[tokens:, :]).astype(BF16)
        cot_ref[i, :, width : 2 * width] = jnp.where(first, acc_v[0:tokens, :], acc_v[tokens:, :]).astype(BF16)

        def d_mid(r0, c):
            rows = pl.ds(r0, big)
            xh = (mid_map[rows, :] - m3) * r3
            d = go_ref[rows, :].astype(F32) + r3 * (dn_ref[rows, :].astype(F32) - n1 - xh * n2)
            xs_ref[pl.ds(r0 + 8, big), :] = d
            return c

        chunks(big, d_mid)
        gx = gx_ref.at[i]
        chunks(big, lambda r0, c: (shifted(gx, r0, big), c)[1])
        return square

    square = lax.fori_loop(0, images, attend, jnp.zeros((8, mid), F32))

    cot = cot_ref[...].reshape(images * tokens, 2 * width)
    own = kv_blocks.shape[1]

    def project(j, c):
        cols = pl.ds(pl.multiple_of(j * big, big), big)
        value = dot_lhs_t(cot, text[:, :, cols].reshape(images * tokens, big)).astype(BF16)
        kv_blocks[:, :, cols] = value.reshape(dp_size, own, big)
        return c

    lax.fori_loop(0, features // big, project, 0)

    def kv_half(m):
        return pl.ds(pl.multiple_of(m * half, half), half)

    kv_sum = Scatter(
        lambda m: kv_blocks.at[:, :, kv_half(m)],
        lambda d, m: kv_blocks[d, :, kv_half(m)].astype(F32),
        kv_out,
        kv_radices,
        kv_refs,
        dp_size,
        mp_size,
    )

    def conv_sum(blocks, out, radices, refs):
        return Scatter(
            lambda m: blocks.at[m],
            lambda d, m: blocks[m, d].astype(F32),
            out,
            radices,
            refs,
            dp_size,
            mp_size,
        )

    one_sum = conv_sum(one_blocks, one_out, last_radices, one_refs)
    two_sum = conv_sum(two_blocks, two_out, conv_radices, two_refs)

    def cut(grad, blocks):
        rows = blocks.shape[2]
        for d in range(n):
            blocks[d % mp_size, d // mp_size] = grad[d * rows : (d + 1) * rows, :].astype(BF16)

    def second(i):
        weight_grad(a_two.at[i], gx_ref.at[i], channels, grad_two)

    def back(i):
        m2, r2 = row_of(i, 0), row_of(i, 1)
        gain, bias = gain_bias(i)
        gx, conv = gx_ref.at[i], c_ref.at[i]

        def d_act(r0, carry):
            s1, s2 = carry
            rows = pl.ds(r0, big)
            d = convolve(gx, wt_two, r0, big).astype(BF16).astype(F32)
            xh = (conv[rows, :] - m2) * r2
            z = xh * gain + bias
            sg = sigmoid(z)
            d = d * (sg * (1.0 + z * (1.0 - sg))) * gain
            h_ref[rows, :] = d
            return s1 + fold(d), s2 + fold(d * xh)

        s1, s2 = chunks(big, d_act, (zero8, zero8))
        n3, n4 = group_mean(s1, count), group_mean(s2, count)

        def d_conv(r0, c):
            rows = pl.ds(r0, big)
            xh = (conv[rows, :] - m2) * r2
            d = r2 * (h_ref[rows, :] - n3 - xh * n4)
            g_one[pl.ds(r0 + S, big), :] = d.astype(BF16)
            return c

        chunks(big, d_conv)

    def first(i):
        weight_grad(a_one.at[i], g_one, 0, grad_one)

    def steps_of(scatter):
        last = len(scatter.radices)
        for j in range(last + 1):
            if j == 0:
                scatter.start(0)
            else:
                scatter.finish(j - 1)
                scatter.start(j)
            yield
        scatter.finish(last)
        yield

    def lanes_total(x):
        return jnp.sum(jnp.sum(x, axis=0, keepdims=True), axis=1, keepdims=True)

    kv_steps = steps_of(kv_sum)
    next(kv_steps)
    for i in range(images):
        second(i)
    cut(grad_two, two_blocks)
    two_steps = steps_of(two_sum)
    next(kv_steps, None)
    next(two_steps, None)
    for i in range(images):
        back(i)
        next(kv_steps, None)
        next(two_steps, None)
        first(i)
        if i + 1 < images:
            next(kv_steps, None)
            next(two_steps, None)
    cut(grad_one, one_blocks)
    one_steps = steps_of(one_sum)
    next(one_steps)
    for _ in kv_steps:
        pass
    for _ in two_steps:
        pass
    for _ in one_steps:
        pass

    lane1 = lax.broadcasted_iota(jnp.int32, (1, 128), 1)
    parts = (
        lanes_total(one_out[...] * one_out[...]),
        lanes_total(two_out[...] * two_out[...]),
        lanes_total(kv_out[...] * kv_out[...]),
        lanes_total(square),
    )
    stat = jnp.zeros((1, 128), F32)
    for k, part in enumerate(parts):
        stat = jnp.where(lane1 == k, part, stat)
    stat_ref[...] = stat

    def stat_copy(k, slot):
        return pltpu.make_async_remote_copy(
            src_ref=stat_ref,
            dst_ref=stat_land.at[slot],
            send_sem=stat_send.at[k],
            recv_sem=stat_recv.at[k],
            device_id=place(target(k)),
            device_id_type=pl.DeviceIdType.MESH,
        )

    over_peers(lambda k: stat_copy(k, me).start())
    stat_land[me] = stat
    over_peers(lambda k: stat_copy(k, lax.rem(me + n - k - 1, n)).wait_recv())
    stat_out[...] = jnp.sum(stat_land[...], axis=0)
    over_peers(lambda k: stat_copy(k, me).wait_send())
    for k in range(mp_size - 1):
        kv_copy(k).wait_send()
    for scatter in (kv_sum, two_sum, one_sum):
        scatter.drain()


def scale_kernel(conv_count, kv_count, loss_count, one, two, kv, stats, one_out, two_out, kv_out, loss_out):
    row = stats[...]
    one_out[...] = one[...] * lax.rsqrt(row[:, 0:1] / conv_count + 1e-06)
    two_out[...] = two[...] * lax.rsqrt(row[:, 1:2] / conv_count + 1e-06)
    kv_out[...] = kv[...] * lax.rsqrt(row[:, 2:3] / kv_count + 1e-06)
    loss_out[...] = row[:, 3:4] / loss_count


def local(
    clean,
    noise,
    lowres,
    aug_noise,
    timesteps,
    aug_levels,
    lengths,
    text,
    w_stem,
    w_time,
    conv_one,
    conv_two,
    kv_weight,
    w_query,
    w_output,
    w_head,
):
    dp_size = lax.axis_size("dp")
    mp_size = lax.axis_size("mp")
    n = dp_size * mp_size
    images, tokens, features = text.shape
    pixels = clean.shape[2]
    channels, width = w_query.shape
    span = TAPS * channels
    half = kv_weight.shape[0]
    own = 2 * width // dp_size
    rows = conv_one.shape[0] // n
    kv_radices = conv_radices = last_radices = radices_of(dp_size)
    turn = lambda x: jnp.transpose(x, (1, 0, 2))
    arrays = (
        turn(clean),
        turn(noise),
        turn(lowres),
        turn(aug_noise),
        text,
        kv_weight,
        w_stem,
        w_time,
        conv_one,
        conv_two,
        w_query,
        w_output,
        w_head,
    )
    vmem = pl.BlockSpec(memory_space=pltpu.VMEM)
    smem = pl.BlockSpec(memory_space=pltpu.SMEM)
    v = pltpu.VMEM
    dma = pltpu.SemaphoreType.DMA
    padded = pixels + 2 * S
    conv_block = (rows, channels)
    one, two, kv, stats = pl.pallas_call(
        functools.partial(block_kernel, n, mp_size, kv_radices, conv_radices, last_radices),
        out_shape=(
            jax.ShapeDtypeStruct(conv_block, F32),
            jax.ShapeDtypeStruct(conv_block, F32),
            jax.ShapeDtypeStruct((own, half), F32),
            jax.ShapeDtypeStruct((1, 128), F32),
        ),
        in_specs=[smem] * 3 + [vmem] * len(arrays),
        out_specs=(vmem,) * 4,
        scratch_shapes=[
            v((images, 8, 2 * channels), F32),
            v((images, tokens, 2 * width), BF16),
            v((images, tokens, 2 * width), BF16),
            v((width, HEADS * tokens), BF16),
            v((HEADS * tokens, width), BF16),
            v((HEADS * tokens, width), BF16),
            v((width, HEADS * tokens), BF16),
            v((width, channels), BF16),
            v((channels, width), BF16),
            v((TAPS * span, channels), BF16),
            v((16, channels), F32),
            v((images, 8, pixels), F32),
            v((images, 8, pixels), F32),
            v((images, 4, 8, channels), F32),
            v((pixels, channels), F32),
            v((pixels + 16, channels), F32),
            v((images, padded, span), BF16),
            v((images, padded, span), BF16),
            v((images, padded, span), BF16),
            v((images, pixels, channels), F32),
            v((images, pixels, channels), F32),
            v((pixels, channels), BF16),
            v((pixels, channels), BF16),
            v((padded, channels), BF16),
            v((span, span), F32),
            v((HEADS * tokens, width), F32),
            v((HEADS * tokens, width), F32),
            v(conv_one.shape, F32),
            v(conv_one.shape, F32),
            v((mp_size - 1,) + kv_weight.shape, BF16),
            dma((mp_size - 1,)),
            dma((mp_size - 1,)),
            v((1, 128), F32),
            v((n, 1, 128), F32),
            dma((n - 1,)),
            dma((n - 1,)),
            v((dp_size, own, features), BF16),
            v((mp_size, dp_size) + conv_block, BF16),
            v((mp_size, dp_size) + conv_block, BF16),
        ]
        + scratch_of((own, half), kv_radices, dp_size, mp_size)
        + scratch_of(conv_block, last_radices, dp_size, mp_size)
        + scratch_of(conv_block, conv_radices, dp_size, mp_size),
        compiler_params=pltpu.CompilerParams(
            collective_id=0, has_side_effects=True, vmem_limit_bytes=62 * 1024 * 1024
        ),
    )(timesteps, aug_levels, lengths, *arrays)
    conv_count = conv_one.shape[0] * conv_one.shape[1]
    kv_count = half * mp_size * 2 * width
    loss_count = images * n * clean.shape[1] * pixels
    one, two, kv, loss = pl.pallas_call(
        functools.partial(scale_kernel, conv_count, kv_count, loss_count),
        out_shape=(
            jax.ShapeDtypeStruct(conv_block, F32),
            jax.ShapeDtypeStruct(conv_block, F32),
            jax.ShapeDtypeStruct((own, half), F32),
            jax.ShapeDtypeStruct((1, 1), F32),
        ),
        in_specs=[vmem] * 4,
        out_specs=(vmem,) * 4,
    )(one, two, kv, stats)
    return (one, two, kv.T, loss.reshape(()))


def solution(mesh):
    return jax.shard_map(
        local,
        mesh=mesh,
        in_specs=(
            P(("dp", "mp"), None, None),
            P(("dp", "mp"), None, None),
            P(("dp", "mp"), None, None),
            P(("dp", "mp"), None, None),
            P(("dp", "mp")),
            P(("dp", "mp")),
            P(("dp", "mp")),
            P(("dp", "mp"), None, None),
            P(),
            P(),
            P(),
            P(),
            P("mp", None),
            P(),
            P(),
            P(),
        ),
        out_specs=(P(("dp", "mp"), None), P(("dp", "mp"), None), P("mp", "dp"), P()),
        check_vma=False,
    )
```

time: 316 us -> 115 us (0.36)
  matrix products: 96.3 us -> 0 us
  local copies, waits for them, and re-layouts: 52.8 us -> 0 us
  other arithmetic: 36.8 us -> 0 us
  Pallas kernels: 82.8 us -> 115 us
  between operations: 16.2 us -> 0.65 us
  waiting for transfers between devices: 15.5 us -> 0 us
  loops' own time: 13.1 us -> 0 us
    dot_general x60 -> x0, matrix products: 54.3 us -> none  [the longest x4 12.1 us: image_loss(): jnp.einsum('kc,pc->kp', w_head, h_out.astype(jnp.bfloat16), preferred_ele...]
    conv_general_dilated x10 -> x0, matrix products: 42 us -> none  [convolve(): lax.conv_general_dilated(picture, kernel, (1, 1), 'SAME', dimension_numbe...]
    pallas_call x1 -> x2, Pallas kernels: 82.8 us -> 115 us  [the longest x1 113 us: local(): pl.pallas_call(functools.partial(block_kernel, n, mp_size, kv_radices, co...]
    reduce_sum x27 -> x0, other arithmetic: 24.1 us -> none  [the longest x4 8.52 us: image_loss(): highest = jnp.max(scores, axis=1, keepdims=True)]
    while x260 -> x0, local copies, waits for them, and re-layouts: 19.4 us -> none
    all_gather x1 -> x0, waiting for transfers between devices: 14.8 us -> none  [local(): piece = lax.all_gather(kv_weight, 'mp', axis=0, tiled=True)]
    another operation x1 -> x0, loops' own time: 13.1 us -> none  [local(): lax.map(one_image, (clean, noise, lowres, aug_noise, timesteps, aug_level...]
    dynamic_slice x14 -> x0, local copies, waits for them, and re-layouts: 11.3 us -> none  [local(): lax.map(one_image, (clean, noise, lowres, aug_noise, timesteps, aug_level...]
  transfers between devices with their start and end apart: 1 -> 0, of which waited for: 1 -> 0; matrix products, arithmetic and copies ran while one was open for 0% -> 0% of each run, Pallas kernels for 0% -> 0%
where the time goes in v1:
time: 115 us
  Pallas kernels  115 us (100%)
    pallas_call x1, Pallas kernels, local(): pl.pallas_call(functools.partial(block_kernel, n, mp_size, kv_radices, co...  113 us

profile of v1, /device:TPU:0, one launch (start us, length us, event | category | flops | bytes accessed | tf_op | source)
XLA Modules:
  0.0 115.3 jit_solution(3974015797014991809)
XLA Ops:
  0.6 112.9 %shard_map.183 = (f32[36,128]{1,0:T(8,128)}, f32[36,128]{1,0:T(8,128)}, f32[16,2048]{1,0:T(8,128)}, f32[1,128]{1,0:T(1,128)}) custom-call(s32[2]{0:T(128)} %refs_0_.1, s32[2]{0:T(128)} %refs_1_.1, s32[2]{0:T(128)} %refs_2_.1, f32[3,2,4096]{2,1,0:T(2,128)} %bitcast.6, f32[3,2,4096]{2,1,0:T(2,128)} %bitcast.7, f32[3,2,4096]{2,1,0:T(2,128)} %bitcast.8, ...), custom_call_target="tpu_custom_call" | custom-call | tf_op jit(solution)/shard_map/pallas_call | solution.py:750
  113.6 1.7 %shard_map.184 = (f32[36,128]{1,0:T(8,128)}, f32[36,128]{1,0:T(8,128)}, f32[16,2048]{1,0:T(8,128)}, f32[1,1]{1,0:T(1,128)}) custom-call(f32[36,128]{1,0:T(8,128)} %get-tuple-element.12.one, f32[36,128]{1,0:T(8,128)} %get-tuple-element.13.two, f32[16,2048]{1,0:T(8,128)} %get-tuple-element.14.kv, f32[1,128]{1,0:T(1,128)} %get-tuple-element.15.stats), custom_call_target="tpu_custom_call" | custom-call | tf_op jit(solution)/shard_map/pallas_call | solution.py:811

commit v2 on v1

--- a/solution.py
+++ b/solution.py
@@ -43,11 +43,10 @@
     return jnp.sum(values.reshape(rows // 8, 8, lanes), axis=0)
 
 
-def group_mean(acc, count):
-    total = jnp.sum(acc, axis=0, keepdims=True)
-    channels = acc.shape[1]
-    total = jnp.broadcast_to(total, acc.shape)
-    lane = lax.broadcasted_iota(jnp.int32, acc.shape, 1)
+def group_avg(row):
+    channels = row.shape[1]
+    total = jnp.broadcast_to(row, (8, channels))
+    lane = lax.broadcasted_iota(jnp.int32, total.shape, 1)
     members = channels // GROUPS
     step = 1
     while step < members:
@@ -55,7 +54,29 @@
         down = pltpu.roll(total, step, 1)
         total = total + jnp.where((lane // step) % 2 == 0, up, down)
         step *= 2
-    return total[0:1] / (count * members)
+    return total[0:1] / members
+
+
+def group_mean(acc, count):
+    return group_avg(jnp.sum(acc, axis=0, keepdims=True) / count)
+
+
+def moments(values, first, carry):
+    center, total, square = carry
+    part = fold(values)
+    here = jnp.sum(part, axis=0, keepdims=True) / values.shape[0]
+    center = jnp.where(first, here, center)
+    d = values - center
+    return center, total + part, square + fold(d * d)
+
+
+def norm_of(carry, count):
+    center, total, square = carry
+    mean = jnp.sum(total, axis=0, keepdims=True) / count
+    within = jnp.sum(square, axis=0, keepdims=True) / count - (mean - center) * (mean - center)
+    average = group_avg(mean)
+    spread = group_avg(within + (mean - average) * (mean - average))
+    return average, lax.rsqrt(spread + EPS)
 
 
 def sigmoid(x):
@@ -82,6 +103,16 @@
     return tuple(parts)
 
 
+def order_of(radices, turned=False):
+    out, stride = [], 1
+    for radix in radices:
+        out.append((radix, stride))
+        stride *= radix
+    if turned and len(out) > 1:
+        out[0], out[1] = out[1], out[0]
+    return tuple(out)
+
+
 def blocks_of(shape, radices):
     return [tuple(reversed(radices[j:])) + tuple(shape) for j in range(len(radices))]
 
@@ -93,7 +124,8 @@
     return lands
 
 
-def scratch_of(shape, radices, dp_size, mp_size):
+def scratch_of(shape, order, dp_size, mp_size):
+    radices = [r for r, _ in order]
     copies = mp_size - 1 + sum(r - 1 for r in radices)
     return (
         [pltpu.VMEM(s, BF16) for s in blocks_of(shape, radices)]
@@ -103,18 +135,16 @@
 
 
 class Scatter:
-    def __init__(self, pick, read, final, radices, refs, dp_size, mp_size):
+    def __init__(self, pick, read, final, order, refs, dp_size, mp_size):
+        radices, strides = zip(*order)
         k = len(radices)
         self.pick, self.read, self.final, self.radices = pick, read, final, radices
         self.sums, self.lands = refs[:k], refs[k : 2 * k + 1]
         self.send, self.recv = refs[2 * k + 1 :]
         self.dp_size, self.mp_size = dp_size, mp_size
         self.dp, self.mp = lax.axis_index("dp"), lax.axis_index("mp")
-        self.place = []
-        stride = 1
-        for radix in radices:
-            self.place.append((lax.rem(lax.div(self.dp, stride), radix), stride))
-            stride *= radix
+        self.strides = strides
+        self.place = [(lax.rem(lax.div(self.dp, t), r), t) for r, t in zip(radices, strides)]
 
     def copies(self, j):
         out = []
@@ -163,8 +193,9 @@
                 left //= s
             at = tuple(at)
             if j == 0:
-                value = self.read(flat, self.mp)
-                lands = [self.lands[0][k, flat] for k in range(self.mp_size - 1)]
+                block = sum(a * t for a, t in zip(at, reversed(self.strides)))
+                value = self.read(block, self.mp)
+                lands = [self.lands[0][k, block] for k in range(self.mp_size - 1)]
             else:
                 digit = self.place[j - 1][0]
                 value = self.sums[j - 1][at + (digit,)].astype(F32)
@@ -174,7 +205,7 @@
             if j < len(self.radices):
                 self.sums[j][at] = value.astype(BF16)
             else:
-                self.final[...] = value
+                self.final(value)
 
     def drain(self):
         for j in range(len(self.radices) + 1):
@@ -182,7 +213,7 @@
                 copy.wait_send()
 
 
-def block_kernel(n, mp_size, kv_radices, conv_radices, last_radices, *refs):
+def block_kernel(n, mp_size, orders, *refs):
     (
         tsteps,
         levels,
@@ -191,7 +222,7 @@
         noise,
         lowres,
         aug_noise,
-        text,
+        text_hbm,
         kv_weight,
         w_stem,
         w_time,
@@ -213,7 +244,9 @@
         vt_ref,
         wq_t,
         wo_t,
-        wt_two,
+        tap_one,
+        tap_two,
+        tap_back,
         wh_ref,
         stem_lhs,
         noise_ref,
@@ -233,6 +266,9 @@
         acc_v,
         grad_one,
         grad_two,
+        text,
+        kv_own,
+        load_sem,
         kv_land,
         kv_send,
         kv_recv,
@@ -243,12 +279,13 @@
         kv_blocks,
         one_blocks,
         two_blocks,
-    ) = refs[:59]
-    rest = refs[59:]
-    sizes = [2 * len(r) + 3 for r in (kv_radices, last_radices, conv_radices)]
-    kv_refs = rest[: sizes[0]]
-    one_refs = rest[sizes[0] : sizes[0] + sizes[1]]
-    two_refs = rest[sizes[0] + sizes[1] :]
+    ) = refs[:64]
+    rest = list(refs[64:])
+    groups = []
+    for order in orders:
+        size = 2 * len(order) + 3
+        groups.append(rest[:size])
+        rest = rest[size:]
 
     images, tokens, features = text.shape
     pixels = clean.shape[2]
@@ -257,9 +294,10 @@
     heads = w_head.shape[0]
     half = kv_weight.shape[0]
     dp_size = n // mp_size
-    big = 1024
-    mid = 1024
+    big = 2048
+    mid = 2048
     count = float(pixels)
+    lines = pixels // S
     my_dp, my_mp = lax.axis_index("dp"), lax.axis_index("mp")
     me = my_dp * mp_size + my_mp
 
@@ -272,6 +310,10 @@
     def target(k):
         return lax.rem(me + k + 1, n)
 
+    text_load = pltpu.make_async_copy(text_hbm, text, load_sem.at[0])
+    own_load = pltpu.make_async_copy(kv_weight, kv_own, load_sem.at[1])
+    text_load.start()
+    own_load.start()
     barrier = pltpu.get_barrier_semaphore()
     over_peers(
         lambda k: pl.semaphore_signal(
@@ -286,11 +328,23 @@
 
     wq_t[...] = w_query[...].astype(F32).T.astype(BF16)
     wo_t[...] = w_output[...].astype(F32).T.astype(BF16)
+    none = jnp.zeros((span, channels), BF16)
+    for taps, weight in ((tap_one, conv_one), (tap_two, conv_two)):
+        for parity in range(2):
+            lanes = slice(parity * channels, (parity + 1) * channels)
+            for j in range(TAPS + 1):
+                dy = j - parity
+                piece = weight[dy * span : (dy + 1) * span, :] if 0 <= dy < TAPS else none
+                taps[j * span : (j + 1) * span, lanes] = piece
     for dy in range(TAPS):
         for dx in range(TAPS):
             src = (TAPS * (TAPS - 1 - dy) + (TAPS - 1 - dx)) * channels
-            dst = (TAPS * dy + dx) * channels
-            wt_two[dst : dst + channels, :] = conv_two[src : src + channels, :].astype(F32).T.astype(BF16)
+            piece = conv_two[src : src + channels, :].astype(F32).T.astype(BF16)
+            for parity in range(2):
+                dst = (dy + parity) * span + dx * channels
+                tap_back[dst : dst + channels, parity * channels : (parity + 1) * channels] = piece
+    tap_back[0:span, channels : 2 * channels] = none
+    tap_back[TAPS * span : (TAPS + 1) * span, 0:channels] = none
     wh_ref[...] = jnp.zeros_like(wh_ref)
     wh_ref[0:heads, :] = w_head[...].astype(F32)
     wh_ref[8 : 8 + heads, :] = w_head[...].astype(F32)
@@ -303,8 +357,8 @@
     edge = jnp.zeros((S, span), BF16)
     for i in range(images):
         for ref in (a_one, a_two, gx_ref):
-            ref[i, 0:S, :] = edge
-            ref[i, S + pixels :, :] = edge
+            ref[i, 0] = edge
+            ref[i, lines + 1] = edge
         t = jnp.full((8, 128), tsteps[i].astype(F32), F32)
         a = jnp.full((8, 128), levels[i].astype(F32), F32)
         signal, aug_signal = level_of(t), level_of(a)
@@ -315,8 +369,8 @@
             noise_ref[i, k : k + 1, :] = row
             stem_lhs[i, k : k + 1, :] = k1 * clean[k, i : i + 1, :] + k2 * row
             stem_lhs[i, heads + k : heads + k + 1, :] = k3 * lowres[k, i : i + 1, :] + k4 * aug_noise[k, i : i + 1, :]
-    g_one[0:S, :] = edge[:, :channels]
-    g_one[S + pixels :, :] = edge[:, :channels]
+    g_one[0] = edge[:, :channels]
+    g_one[lines + 1] = edge[:, :channels]
     grad_one[...] = jnp.zeros_like(grad_one)
     grad_two[...] = jnp.zeros_like(grad_two)
 
@@ -334,8 +388,6 @@
     for i in range(images):
         emb_ref[i] = jnp.broadcast_to(emb[i : i + 1], emb.shape)
 
-    pl.semaphore_wait(barrier, n - 1)
-
     def kv_copy(k):
         return pltpu.make_async_remote_copy(
             src_ref=kv_weight,
@@ -346,8 +398,10 @@
             device_id_type=pl.DeviceIdType.MESH,
         )
 
-    for k in range(mp_size - 1):
-        kv_copy(k).start()
+    def fetch():
+        pl.semaphore_wait(barrier, n - 1)
+        for k in range(mp_size - 1):
+            kv_copy(k).start()
 
     def shifted(dst, r0, size):
         x = lax.broadcasted_iota(jnp.int32, (size, channels), 0) % S
@@ -355,26 +409,38 @@
         left = window[7 : 7 + size, :]
         here = window[8 : 8 + size, :]
         right = window[9 : 9 + size, :]
-        rows = pl.ds(r0 + S, size)
-        dst[rows, 0:channels] = jnp.where(x == 0, 0.0, left).astype(BF16)
-        dst[rows, channels : 2 * channels] = here.astype(BF16)
-        dst[rows, 2 * channels : span] = jnp.where(x == S - 1, 0.0, right).astype(BF16)
-
-    def convolve(src, weight, r0, size):
-        total = None
-        for dy in range(TAPS):
-            part = dot(src[pl.ds(r0 + dy * S, size), :], weight[dy * span : (dy + 1) * span, :])
-            total = part if total is None else total + part
-        return total
+        rows = pl.ds(r0 // S + 1, size // S)
+        shape = (size // S, S, channels)
+        dst[rows, :, 0:channels] = jnp.where(x == 0, 0.0, left).astype(BF16).reshape(shape)
+        dst[rows, :, channels : 2 * channels] = here.astype(BF16).reshape(shape)
+        dst[rows, :, 2 * channels : span] = jnp.where(x == S - 1, 0.0, right).astype(BF16).reshape(shape)
+
+    def convolve(src, taps, r0, size):
+        y0 = r0 // S
+        pairs = size // S // 2
+        pieces = [
+            jnp.concatenate([src[y0 + 2 * t + j] for t in range(pairs)], axis=0) for j in range(TAPS + 1)
+        ]
+        out = dot(jnp.concatenate(pieces, axis=1), taps[...])
+        rows = []
+        for t in range(pairs):
+            for parity in range(2):
+                rows.append(out[t * S : (t + 1) * S, parity * channels : (parity + 1) * channels])
+        return jnp.concatenate(rows, axis=0)
 
     def weight_grad(src, g_src, lane0, grad):
         acc_w[...] = jnp.zeros_like(acc_w)
 
         def body(r0, carry):
+            y0 = r0 // S
             g = jnp.concatenate(
-                [g_src[pl.ds(r0 + (2 - dy) * S, big), lane0 : lane0 + channels] for dy in range(TAPS)], axis=1
+                [
+                    g_src[pl.ds(y0 + 2 - dy, big // S), :, lane0 : lane0 + channels].reshape(big, channels)
+                    for dy in range(TAPS)
+                ],
+                axis=1,
             )
-            acc_w[...] += dot_lhs_t(src[pl.ds(r0 + S, big), :], g)
+            acc_w[...] += dot_lhs_t(src[pl.ds(y0 + 1, big // S)].reshape(big, span), g)
             return carry
 
         chunks(big, body)
@@ -382,12 +448,7 @@
             part = acc_w[:, dy * channels : (dy + 1) * channels]
             grad[dy * span : (dy + 1) * span, :] += part.astype(BF16).astype(F32)
 
-    def variance(ref, mean):
-        def body(r0, acc):
-            d = ref[pl.ds(r0, big), :] - mean
-            return acc + fold(d * d)
-
-        return lax.rsqrt(group_mean(chunks(big, body, zero8), count) + EPS)
+    start_sums = (jnp.zeros((1, channels), F32), zero8, zero8)
 
     def keep_row(i, k, value):
         norms[i, k] = jnp.broadcast_to(value, (8, channels))
@@ -399,15 +460,16 @@
         return 1.0 + emb_ref[i, 0:1, 0:channels], emb_ref[i, 0:1, channels : 2 * channels]
 
     def forward(i, carry):
+        pl.when(i == images - 1)(fetch)
+
         def stem(r0, acc):
             x1, x2, x3 = split3(stem_lhs[i, :, pl.ds(r0, big)])
             x = jnp.concatenate([x1, x1, x2, x2, x1, x3], axis=0).astype(BF16)
             h = dot_lhs_t(x, stem_w)
             h_ref[pl.ds(r0, big), :] = h
-            return acc + fold(h)
-
-        m1 = group_mean(chunks(big, stem, zero8), count)
-        r1 = variance(h_ref, m1)
+            return moments(h, r0 == 0, acc)
+
+        m1, r1 = norm_of(chunks(big, stem, start_sums), count)
 
         def act_one(r0, c):
             x = (h_ref[pl.ds(r0, big), :] - m1) * r1
@@ -419,12 +481,11 @@
         chunks(big, lambda r0, c: (shifted(one, r0, big), c)[1])
 
         def conv1(r0, acc):
-            c = convolve(one, conv_one, r0, big)
+            c = convolve(one, tap_one, r0, big)
             conv[pl.ds(r0, big), :] = c
-            return acc + fold(c)
-
-        m2 = group_mean(chunks(big, conv1, zero8), count)
-        r2 = variance(conv, m2)
+            return moments(c, r0 == 0, acc)
+
+        m2, r2 = norm_of(chunks(big, conv1, start_sums), count)
         gain, bias = gain_bias(i)
 
         def act_two(r0, c):
@@ -436,12 +497,11 @@
         chunks(big, lambda r0, c: (shifted(two, r0, big), c)[1])
 
         def conv2(r0, acc):
-            h = h_ref[pl.ds(r0, big), :] + convolve(two, conv_two, r0, big)
+            h = h_ref[pl.ds(r0, big), :] + convolve(two, tap_two, r0, big)
             mid_map[pl.ds(r0, big), :] = h
-            return acc + fold(h)
-
-        m3 = group_mean(chunks(big, conv2, zero8), count)
-        r3 = variance(mid_map, m3)
+            return moments(h, r0 == 0, acc)
+
+        m3, r3 = norm_of(chunks(big, conv2, start_sums), count)
         for k, value in enumerate((m2, r2, m3, r3)):
             keep_row(i, k, value)
         return carry
@@ -452,7 +512,9 @@
         cols = pl.ds(pl.multiple_of(m * half, half), half)
         return text[:, :, cols].reshape(images * tokens, half)
 
-    kv = dot(features_of(my_mp), kv_weight[...])
+    text_load.wait()
+    own_load.wait()
+    kv = dot(features_of(my_mp), kv_own[...])
     for k in range(mp_size - 1):
         kv_copy(k).wait_recv()
         kv += dot(features_of(lax.rem(my_mp + mp_size - k - 1, mp_size)), kv_land[k])
@@ -548,32 +610,43 @@
 
     lax.fori_loop(0, features // big, project, 0)
 
-    def kv_half(m):
-        return pl.ds(pl.multiple_of(m * half, half), half)
-
-    kv_sum = Scatter(
-        lambda m: kv_blocks.at[:, :, kv_half(m)],
-        lambda d, m: kv_blocks[d, :, kv_half(m)].astype(F32),
-        kv_out,
-        kv_radices,
-        kv_refs,
-        dp_size,
-        mp_size,
-    )
-
-    def conv_sum(blocks, out, radices, refs):
+    colors = len(orders) - 2
+    lane_step = half // colors
+
+    def kv_part(m, c):
+        return pl.ds(pl.multiple_of(m * half + c * lane_step, lane_step), lane_step)
+
+    def kv_sum(c):
+        def final(value):
+            kv_out[:, c * lane_step : (c + 1) * lane_step] = value
+
+        return Scatter(
+            lambda m: kv_blocks.at[:, :, kv_part(m, c)],
+            lambda d, m: kv_blocks[d, :, kv_part(m, c)].astype(F32),
+            final,
+            orders[c],
+            groups[c],
+            dp_size,
+            mp_size,
+        )
+
+    def conv_sum(blocks, out, k):
+        def final(value):
+            out[...] = value
+
         return Scatter(
             lambda m: blocks.at[m],
             lambda d, m: blocks[m, d].astype(F32),
-            out,
-            radices,
-            refs,
+            final,
+            orders[k],
+            groups[k],
             dp_size,
             mp_size,
         )
 
-    one_sum = conv_sum(one_blocks, one_out, last_radices, one_refs)
-    two_sum = conv_sum(two_blocks, two_out, conv_radices, two_refs)
+    kv_sums = [kv_sum(c) for c in range(colors)]
+    two_sum = conv_sum(two_blocks, two_out, colors)
+    one_sum = conv_sum(one_blocks, one_out, colors + 1)
 
     def cut(grad, blocks):
         rows = blocks.shape[2]
@@ -583,7 +656,7 @@
     def second(i):
         weight_grad(a_two.at[i], gx_ref.at[i], channels, grad_two)
 
-    def back(i):
+    def back(i, between):
         m2, r2 = row_of(i, 0), row_of(i, 1)
         gain, bias = gain_bias(i)
         gx, conv = gx_ref.at[i], c_ref.at[i]
@@ -591,7 +664,7 @@
         def d_act(r0, carry):
             s1, s2 = carry
             rows = pl.ds(r0, big)
-            d = convolve(gx, wt_two, r0, big).astype(BF16).astype(F32)
+            d = convolve(gx, tap_back, r0, big).astype(BF16).astype(F32)
             xh = (conv[rows, :] - m2) * r2
             z = xh * gain + bias
             sg = sigmoid(z)
@@ -601,12 +674,13 @@
 
         s1, s2 = chunks(big, d_act, (zero8, zero8))
         n3, n4 = group_mean(s1, count), group_mean(s2, count)
+        between()
 
         def d_conv(r0, c):
             rows = pl.ds(r0, big)
             xh = (conv[rows, :] - m2) * r2
             d = r2 * (h_ref[rows, :] - n3 - xh * n4)
-            g_one[pl.ds(r0 + S, big), :] = d.astype(BF16)
+            g_one[pl.ds(r0 // S + 1, big // S)] = d.astype(BF16).reshape(big // S, S, channels)
             return c
 
         chunks(big, d_conv)
@@ -615,32 +689,30 @@
         weight_grad(a_one.at[i], g_one, 0, grad_one)
 
     def steps_of(scatter):
-        last = len(scatter.radices)
-        for j in range(last + 1):
-            if j == 0:
-                scatter.start(0)
-            else:
-                scatter.finish(j - 1)
-                scatter.start(j)
+        group = scatter if isinstance(scatter, list) else [scatter]
+        last = len(group[0].radices)
+        for j in range(last + 2):
+            for one in group:
+                if j > 0:
+                    one.finish(j - 1)
+                if j <= last:
+                    one.start(j)
             yield
-        scatter.finish(last)
-        yield
 
     def lanes_total(x):
         return jnp.sum(jnp.sum(x, axis=0, keepdims=True), axis=1, keepdims=True)
 
-    kv_steps = steps_of(kv_sum)
+    kv_steps = steps_of(kv_sums)
+    two_steps = steps_of(two_sum)
     next(kv_steps)
     for i in range(images):
         second(i)
+        if i == 0:
+            next(kv_steps, None)
     cut(grad_two, two_blocks)
-    two_steps = steps_of(two_sum)
-    next(kv_steps, None)
-    next(two_steps, None)
+    next(two_steps)
     for i in range(images):
-        back(i)
-        next(kv_steps, None)
-        next(two_steps, None)
+        back(i, lambda: (next(kv_steps, None), next(two_steps, None)))
         first(i)
         if i + 1 < images:
             next(kv_steps, None)
@@ -684,7 +756,7 @@
     over_peers(lambda k: stat_copy(k, me).wait_send())
     for k in range(mp_size - 1):
         kv_copy(k).wait_send()
-    for scatter in (kv_sum, two_sum, one_sum):
+    for scatter in (*kv_sums, two_sum, one_sum):
         scatter.drain()
 
 
@@ -724,7 +796,14 @@
     half = kv_weight.shape[0]
     own = 2 * width // dp_size
     rows = conv_one.shape[0] // n
-    kv_radices = conv_radices = last_radices = radices_of(dp_size)
+    radices = radices_of(dp_size)
+    orders = (
+        order_of(radices),
+        order_of(radices, turned=True),
+        order_of(radices),
+        order_of((dp_size,)),
+    )
+    kv_block = (own, half // (len(orders) - 2))
     turn = lambda x: jnp.transpose(x, (1, 0, 2))
     arrays = (
         turn(clean),
@@ -743,19 +822,20 @@
     )
     vmem = pl.BlockSpec(memory_space=pltpu.VMEM)
     smem = pl.BlockSpec(memory_space=pltpu.SMEM)
+    hbm = pl.BlockSpec(memory_space=pl.ANY)
     v = pltpu.VMEM
     dma = pltpu.SemaphoreType.DMA
-    padded = pixels + 2 * S
+    lines = pixels // S + 2
     conv_block = (rows, channels)
     one, two, kv, stats = pl.pallas_call(
-        functools.partial(block_kernel, n, mp_size, kv_radices, conv_radices, last_radices),
+        functools.partial(block_kernel, n, mp_size, orders),
         out_shape=(
             jax.ShapeDtypeStruct(conv_block, F32),
             jax.ShapeDtypeStruct(conv_block, F32),
             jax.ShapeDtypeStruct((own, half), F32),
             jax.ShapeDtypeStruct((1, 128), F32),
         ),
-        in_specs=[smem] * 3 + [vmem] * len(arrays),
+        in_specs=[smem] * 3 + [vmem] * 4 + [hbm] * 2 + [vmem] * (len(arrays) - 6),
         out_specs=(vmem,) * 4,
         scratch_shapes=[
             v((images, 8, 2 * channels), F32),
@@ -767,26 +847,31 @@
             v((width, HEADS * tokens), BF16),
             v((width, channels), BF16),
             v((channels, width), BF16),
-            v((TAPS * span, channels), BF16),
+            v(((TAPS + 1) * span, 2 * channels), BF16),
+            v(((TAPS + 1) * span, 2 * channels), BF16),
+            v(((TAPS + 1) * span, 2 * channels), BF16),
             v((16, channels), F32),
             v((images, 8, pixels), F32),
             v((images, 8, pixels), F32),
             v((images, 4, 8, channels), F32),
             v((pixels, channels), F32),
             v((pixels + 16, channels), F32),
-            v((images, padded, span), BF16),
-            v((images, padded, span), BF16),
-            v((images, padded, span), BF16),
+            v((images, lines, S, span), BF16),
+            v((images, lines, S, span), BF16),
+            v((images, lines, S, span), BF16),
             v((images, pixels, channels), F32),
             v((images, pixels, channels), F32),
             v((pixels, channels), BF16),
             v((pixels, channels), BF16),
-            v((padded, channels), BF16),
+            v((lines, S, channels), BF16),
             v((span, span), F32),
             v((HEADS * tokens, width), F32),
             v((HEADS * tokens, width), F32),
             v(conv_one.shape, F32),
             v(conv_one.shape, F32),
+            v(text.shape, BF16),
+            v(kv_weight.shape, BF16),
+            dma((2,)),
             v((mp_size - 1,) + kv_weight.shape, BF16),
             dma((mp_size - 1,)),
             dma((mp_size - 1,)),
@@ -798,9 +883,13 @@
             v((mp_size, dp_size) + conv_block, BF16),
             v((mp_size, dp_size) + conv_block, BF16),
         ]
-        + scratch_of((own, half), kv_radices, dp_size, mp_size)
-        + scratch_of(conv_block, last_radices, dp_size, mp_size)
-        + scratch_of(conv_block, conv_radices, dp_size, mp_size),
+        + sum(
+            (
+                scratch_of(kv_block if c < len(orders) - 2 else conv_block, order, dp_size, mp_size)
+                for c, order in enumerate(orders)
+            ),
+            [],
+        ),
         compiler_params=pltpu.CompilerParams(
             collective_id=0, has_side_effects=True, vmem_limit_bytes=62 * 1024 * 1024
         ),

time: 115 us -> 86.1 us (0.75)
  Pallas kernels: 115 us -> 85.3 us
    pallas_call x1, Pallas kernels: 113 us -> 83.6 us  [local(): pl.pallas_call(functools.partial(block_kernel, n, mp_size, orders), out_s...]
where the time goes in v2:
time: 86.1 us; the launch traced here: 85.9 us
  Pallas kernels  85.3 us (99%)
    pallas_call x1, Pallas kernels, local(): pl.pallas_call(functools.partial(block_kernel, n, mp_size, orders), out_s...  83.6 us

profile of v2, /device:TPU:0, one launch (start us, length us, event | category | flops | bytes accessed | tf_op | source)
XLA Modules:
  0.0 85.9 jit_solution(12352047816275668244)
XLA Ops:
  0.6 83.6 %shard_map.183 = (f32[36,128]{1,0:T(8,128)}, f32[36,128]{1,0:T(8,128)}, f32[16,2048]{1,0:T(8,128)}, f32[1,128]{1,0:T(1,128)}) custom-call(s32[2]{0:T(128)} %refs_0_.1, s32[2]{0:T(128)} %refs_1_.1, s32[2]{0:T(128)} %refs_2_.1, f32[3,2,4096]{2,1,0:T(2,128)} %bitcast.6, f32[3,2,4096]{2,1,0:T(2,128)} %bitcast.7, f32[3,2,4096]{2,1,0:T(2,128)} %bitcast.8, ...), custom_call_target="tpu_custom_call" | custom-call | tf_op jit(solution)/shard_map/pallas_call | solution.py:830
  84.2 1.7 %shard_map.184 = (f32[36,128]{1,0:T(8,128)}, f32[36,128]{1,0:T(8,128)}, f32[16,2048]{1,0:T(8,128)}, f32[1,1]{1,0:T(1,128)}) custom-call(f32[36,128]{1,0:T(8,128)} %get-tuple-element.12.one, f32[36,128]{1,0:T(8,128)} %get-tuple-element.13.two, f32[16,2048]{1,0:T(8,128)} %get-tuple-element.14.kv, f32[1,128]{1,0:T(1,128)} %get-tuple-element.15.stats), custom_call_target="tpu_custom_call" | custom-call | tf_op jit(solution)/shard_map/pallas_call | solution.py:900
